TPU v7x, 16 devices: a whole 2x2x2 slice. The times are simulated.
16 devices in a mesh: dp: 4 (over z, y), sp: 4 (over x, core).
Axes of the slice: x: 2, y: 2, z: 2, core: 2. Of those that a mesh axis runs over, the one named last changes fastest.
Arguments:
- hidden: bfloat16 [64, 1024, 768], P('dp', 'sp'), parts along dimension 0
- pos_ids: int32 [64, 1024], P('dp', 'sp'), parts along dimension 0
- block_ids: int32 [64, 1024], P('dp', 'sp'), parts along dimension 0
- ctx_len: int32 [64], P('dp'), parts along dimension 0
- ln_gamma: bfloat16 [768], replicated
- ln_beta: bfloat16 [768], replicated
- w_qkv: bfloat16 [768, 12, 3, 64], replicated
- b_qkv: bfloat16 [12, 3, 64], replicated
- w_dense: bfloat16 [768, 768], replicated
- b_dense: bfloat16 [768], replicated
Outputs:
- output 1: bfloat16 [64, 1024, 768], P('dp', 'sp'), parts along dimension 0
- output 2: bfloat16 [64, 1024, 12, 64], P('dp', None, 'sp'), parts along dimension 0
- output 3: bfloat16 [64, 1024, 12, 64], P('dp', None, 'sp'), parts along dimension 0
There are 4 independent parts. A program takes and returns all parts, laid end to end along the dimension named above; an argument that names none is the same for every part.
All inputs are finite; a program needn't handle non-finite values.
Results may differ from a plain program's by a relative error of at most 0.00594918.
Values are sent between devices in bfloat16 or wider.
A program may use at most 1 GiB of HBM per device.

v0:
```python
import math
import jax
import jax.numpy as jnp
from jax import lax
from jax.sharding import PartitionSpec as P

ALPHA = math.sqrt(56.0)
ROPE_BASE = 10000.0
LN_EPS = 1e-5
SCORE_BUDGET = 2 ** 25


def layer_norm(hidden, ln_gamma, ln_beta):
    wide_in = hidden.astype(jnp.float32)
    row_mean = jnp.mean(wide_in, axis=-1, keepdims=True)
    centered = wide_in - row_mean
    row_var = jnp.mean(jnp.square(centered), axis=-1, keepdims=True)
    return (centered * lax.rsqrt(row_var + LN_EPS) * ln_gamma.astype(jnp.float32) + ln_beta.astype(jnp.float32)).astype(jnp.bfloat16)


def rotate_pairs(qk_pair, pos_ids, block_ids):
    half_dim = qk_pair.shape[-1] // 2
    quarter_dim = half_dim // 2
    inv_freq = ROPE_BASE ** (-jnp.arange(0, half_dim, 2).astype(jnp.float32) / half_dim)
    angles = jnp.stack([pos_ids, block_ids], axis=-1).astype(jnp.float32)[..., None] * inv_freq
    cos_a = jnp.cos(angles)[:, :, None, None]
    sin_a = jnp.sin(angles)[:, :, None, None]
    split_dims = qk_pair.astype(jnp.float32).reshape(qk_pair.shape[:-1] + (2, 2, quarter_dim))
    low_part = split_dims[..., 0, :]
    high_part = split_dims[..., 1, :]
    new_low = low_part * cos_a - high_part * sin_a
    new_high = high_part * cos_a + low_part * sin_a
    return jnp.stack([new_low, new_high], axis=-2).reshape(qk_pair.shape).astype(jnp.bfloat16)


def query_block(cell_count, query_len, key_len):
    block_len = query_len
    while block_len % 2 == 0 and block_len > 8 and cell_count * block_len * key_len > SCORE_BUDGET:
        block_len = block_len // 2
    return block_len


def attend(query_rot, key_heads, value_heads, ctx_len, q_offset):
    row_count, query_len, head_count, head_dim = query_rot.shape
    key_len = key_heads.shape[1]
    block_len = query_block(row_count * head_count, query_len, key_len)
    score_scale = 1.0 / math.sqrt(head_dim)
    key_pos = jnp.arange(key_len)
    ctx_visible = (key_pos[None, :] < ctx_len[:, None])[:, None, None, :]

    def attend_block(block_idx, context):
        block_start = block_idx * block_len
        q_block = lax.dynamic_slice_in_dim(query_rot, block_start, block_len, axis=1)
        scores = jnp.einsum('bqhe,bkhe->bhqk', q_block, key_heads, preferred_element_type=jnp.float32) * score_scale
        q_pos = q_offset + block_start + jnp.arange(block_len)
        visible = ctx_visible | (key_pos[None, None, None, :] <= q_pos[None, None, :, None])
        attn_probs = jax.nn.softmax(jnp.where(visible, scores, -jnp.inf), axis=-1).astype(jnp.bfloat16)
        block_out = jnp.einsum('bhqk,bkhe->bqhe', attn_probs, value_heads, preferred_element_type=jnp.float32).astype(jnp.bfloat16)
        return lax.dynamic_update_slice_in_dim(context, block_out, block_start, axis=1)

    return lax.fori_loop(0, query_len // block_len, attend_block, jnp.zeros_like(query_rot))


def solution(mesh):
    seq_spec = P('dp', 'sp', None)
    row_spec = P('dp', 'sp')
    head_spec = P('dp', None, 'sp', None)
    replicated = P()

    def local_block(hidden, pos_ids, block_ids, ctx_len, ln_gamma, ln_beta, w_qkv, b_qkv, w_dense, b_dense):
        normed = layer_norm(hidden, ln_gamma, ln_beta)
        qkv_proj = (jnp.einsum('bsd,dhte->bshte', normed, w_qkv, preferred_element_type=jnp.float32) + b_qkv.astype(jnp.float32)).astype(jnp.bfloat16)
        qk_rot = rotate_pairs(qkv_proj[:, :, :, :2], pos_ids, block_ids)
        qkv_rot = jnp.concatenate([qk_rot, qkv_proj[:, :, :, 2:]], axis=3)
        by_heads = lax.all_to_all(qkv_rot, 'sp', 2, 1, tiled=True)
        key_heads = by_heads[:, :, :, 1]
        value_heads = by_heads[:, :, :, 2]
        context = attend(by_heads[:, :, :, 0], key_heads, value_heads, ctx_len, 0)
        by_tokens = lax.all_to_all(context, 'sp', 1, 2, tiled=True)
        head_count, head_dim = by_tokens.shape[2], by_tokens.shape[3]
        dense_out = jnp.einsum('bshe,hef->bsf', by_tokens, w_dense.reshape(head_count, head_dim, -1), preferred_element_type=jnp.float32)
        block_out = (normed.astype(jnp.float32) * ALPHA + dense_out + b_dense.astype(jnp.float32)).astype(jnp.bfloat16)
        return block_out, key_heads, value_heads

    return jax.shard_map(local_block, mesh=mesh, in_specs=(seq_spec, row_spec, row_spec, P('dp'), replicated, replicated, replicated, replicated, replicated, replicated), out_specs=(seq_spec, head_spec, head_spec), check_vma=False)
```

profile of v0, /device:TPU:0, one launch (start us, length us, event | category | flops | bytes accessed | tf_op | source)
XLA Modules:
  0.0 682.6 jit_solution(5676236792537518301)
XLA Ops:
  1.2 3.7 convert_reduce_fusion
  4.9 4.7 fusion.28
  9.7 0.6 add_rsqrt_fusion
  11.5 0.6 convert_element_type.68
  12.1 21.4 %add_convert_fusion = bf16[16,256,12,3,64]{1,4,3,2,0:T(8,128)(2,1)} fusion(f32[12,3,64]{2,1,0:T(4,128)} %convert_element_type.68, bf16[768,12,3,64]{0,3,2,1:T(8,128)(2,1)S(1)} %copy-done, bf16[16,256,768]{2,1,0:T(8,128)(2,1)} %param.12, f32[768]{0:T(1024)} %convert_element_type.65, f32[768]{0:T(1024)} %convert_element_type.64, ...), kind=kOutput, calls=%fused_computation.25 | convolution fusion | flops 14533263360 | bytes 28752896 | tf_op jit(solution)/shard_map/bsd,dhte->bshte/dot_general | solution.py:72
  33.5 4.6 slice-done
  38.1 9.1 %convert.9 = f32[16,256,12,2,2,2,16]{1,6,5,4,3,2,0:T(8,128)} convert(bf16[16,256,12,2,2,2,16]{1,6,5,4,3,2,0:T(8,128)(2,1)S(1)} %bitcast.60) | non-fusion elementwise | flops 6291456 | bytes 37748736 | tf_op jit(solution)/shard_map/reshape | solution.py:28
  47.3 1.9 multiply_cosine_fusion
  49.2 10.9 %subtract_convert_fusion = (bf16[16,256,12,2,2,1,16]{1,6,5,4,3,2,0:T(8,128)(2,1)S(1)}, bf16[16,256,12,2,2,1,16]{1,6,5,4,3,2,0:T(8,128)(2,1)S(1)}) fusion(f32[16,256,12,2,2,2,16]{1,6,5,4,3,2,0:T(8,128)} %convert.9, f32[16,256,2,16]{1,3,2,0:T(8,128)S(1)} %get-tuple-element.164, f32[16,256,2,16]{1,3,2,0:T(8,128)S(1)} %get-tuple-element.163), kind=kLoop, calls=%fused_computation.40 | loop fusion | flops 25165824 | bytes 38797312 | tf_op jit(solution)/shard_map/convert.1
  60.1 1.2 pad_maximum_fusion.1
  61.3 1.8 copy.28
  63.1 10.6 %pad_maximum_fusion = bf16[16,256,12,3,64]{1,4,3,0,2:T(8,128)(2,1)} fusion(bf16[16,256,12,2,64]{1,4,3,0,2:T(8,128)(2,1)S(1)} %bitcast.59, bf16[16,256,12,3,64]{1,4,3,2,0:T(8,128)(2,1)} %add_convert_fusion), kind=kLoop, calls=%fused_computation.26 | loop fusion | flops 37748736 | bytes 37748736 | tf_op jit(solution)/shard_map/concatenate | solution.py:74
  73.6 7.3 %all-to-all-start = ((bf16[16,256,12,3,64]{1,4,3,0,2:T(8,128)(2,1)}), bf16[16,256,12,3,64]{1,4,3,0,2:T(8,128)(2,1)}, u32[]{:S(2)}, u32[]{:S(2)}) async-start(bf16[16,256,12,3,64]{1,4,3,0,2:T(8,128)(2,1)} %pad_maximum_fusion), calls=%async_computation | async-start | bytes 37748736 | tf_op jit(solution)/shard_map/all_to_all | solution.py:75
  81.0 206.1 %all-to-all-done = bf16[16,256,12,3,64]{1,4,3,0,2:T(8,128)(2,1)} async-done(((bf16[16,256,12,3,64]{1,4,3,0,2:T(8,128)(2,1)}), bf16[16,256,12,3,64]{1,4,3,0,2:T(8,128)(2,1)}, u32[]{:S(2)}, u32[]{:S(2)}) %all-to-all-start) | async-done | bytes 18874400 | tf_op jit(solution)/shard_map/all_to_all | solution.py:75
  287.1 24.8 %copy.31 = bf16[16,4,256,3,3,64]{2,1,5,4,3,0:T(4,128)(2,1)} copy(bf16[16,4,256,3,3,64]{2,5,4,0,3,1:T(8,128)(2,1)} %bitcast.10) | data formatting | bytes 37748736 | tf_op jit(solution)/shard_map/all_to_all | solution.py:75
  311.9 30.7 %all_to_all.29 = bf16[16,1024,3,3,64]{1,4,3,2,0:T(8,128)(2,1)} reshape(bf16[16,4,256,3,3,64]{2,1,5,4,3,0:T(4,128)(2,1)} %copy.31) | data formatting | bytes 37748736 | tf_op jit(solution)/shard_map/all_to_all | solution.py:75
  342.5 15.4 %slice_bitcast_fusion = (bf16[16,1024,3,64]{1,3,2,0:T(8,128)(2,1)}, bf16[16,1024,3,64]{1,3,2,0:T(8,128)(2,1)}, bf16[16,1024,3,64]{1,3,2,0:T(8,128)(2,1)}) fusion(bf16[16,1024,3,3,64]{1,4,3,2,0:T(8,128)(2,1)} %all_to_all.29), kind=kLoop, calls=%fused_computation.41 | loop fusion | bytes 37748736 | tf_op jit(solution)/shard_map/squeeze | solution.py:77
  357.9 3.5 broadcast_in_dim.54
  361.5 177.3 %while.14 = (s32[]{:T(128)}, bf16[16,1024,3,64]{1,3,2,0:T(8,128)(2,1)}, bf16[16,1024,3,64]{1,3,2,0:T(8,128)(2,1)}, bf16[16,1024,3,64]{1,3,2,0:T(8,128)(2,1)}, bf...) while((s32[]{:T(128)}, ...), condition=%wide.region_5.6_spmd.clone, body=%wide.region_2.5_spmd.clone.sunk | while | flops 6603949568 | bytes 238260752 | solution.py:61
  361.9 7.9 %broadcast_or_fusion.2 = pred[16,512,1024]{2,1,0:T(8,128)(4,1)} fusion(pred[512,1024]{1,0:T(8,128)(4,1)S(1)} %iota_compare_fusion.3, pred[16,1024]{1,0:T(8,128)(4,1)S(1)} %fusion.57), kind=kLoop, calls=%fused_computation.12.clone.1 | loop fusion | flops 8388608 | bytes 8929280 | tf_op jit(solution)/shard_map/while/body/eval_jaxpr/or | solution.py:56
  369.8 43.9 %fusion.58 = (f32[16,3,512]{2,1,0:T(4,128)S(1)}, f32[16,3,512,1024]{3,2,1,0:T(8,128)}) fusion(bf16[16,1024,3,64]{1,3,2,0:T(8,128)(2,1)} %get-tuple-element.229, pred[16,512,1024]{2,1,0:T(8,128)(4,1)} %broadcast_or_fusion.2, bf16[16,1024,3,64]{1,3,2,0:T(8,128)(2,1)} %get-tuple-element.228, s32[]{:T(128)S(6)} %select_n.31), kind=kOutput, calls=%fused_computation.52.clone.1 | convolution fusion | flops 3321889792 | bytes 118587392 | tf_op jit(solution)/shard_map/while/body/eval_jaxpr/sub | solution.py:57
  413.7 36.2 %bitcast_dynamic-update-slice_fusion.2 = bf16[16,1024,3,64]{1,3,2,0:T(8,128)(2,1)} fusion(bf16[16,1024,3,64]{1,3,2,0:T(8,128)(2,1)} %get-tuple-element.217, s32[]{:T(128)S(6)} %select_n.31, bf16[16,1024,3,64]{1,3,2,0:T(8,128)(2,1)} %get-tuple-element.230, f32[16,3,512,1024]{3,2,1,0:T(8,128)} %get-tuple-element.204, ...), kind=kOutput, calls=%fused_computation.13.clone.1 | convolution fusion | flops 3273129984 | bytes 110198784 | tf_op jit(solution)/shard_map/while/body/eval_jaxpr/bhqk,bkhe->bqhe/dot_general | solution.py:58
  450.4 7.9 %broadcast_or_fusion.2 = pred[16,512,1024]{2,1,0:T(8,128)(4,1)} fusion(pred[512,1024]{1,0:T(8,128)(4,1)S(1)} %iota_compare_fusion.3, pred[16,1024]{1,0:T(8,128)(4,1)S(1)} %fusion.57), kind=kLoop, calls=%fused_computation.12.clone.1 | loop fusion | flops 8388608 | bytes 8929280 | tf_op jit(solution)/shard_map/while/body/eval_jaxpr/or | solution.py:56
  458.3 44.3 %fusion.58 = (f32[16,3,512]{2,1,0:T(4,128)S(1)}, f32[16,3,512,1024]{3,2,1,0:T(8,128)}) fusion(bf16[16,1024,3,64]{1,3,2,0:T(8,128)(2,1)} %get-tuple-element.229, pred[16,512,1024]{2,1,0:T(8,128)(4,1)} %broadcast_or_fusion.2, bf16[16,1024,3,64]{1,3,2,0:T(8,128)(2,1)} %get-tuple-element.228, s32[]{:T(128)S(6)} %select_n.31), kind=kOutput, calls=%fused_computation.52.clone.1 | convolution fusion | flops 3321889792 | bytes 118587392 | tf_op jit(solution)/shard_map/while/body/eval_jaxpr/sub | solution.py:57
  502.6 36.2 %bitcast_dynamic-update-slice_fusion.2 = bf16[16,1024,3,64]{1,3,2,0:T(8,128)(2,1)} fusion(bf16[16,1024,3,64]{1,3,2,0:T(8,128)(2,1)} %get-tuple-element.217, s32[]{:T(128)S(6)} %select_n.31, bf16[16,1024,3,64]{1,3,2,0:T(8,128)(2,1)} %get-tuple-element.230, f32[16,3,512,1024]{3,2,1,0:T(8,128)} %get-tuple-element.204, ...), kind=kOutput, calls=%fused_computation.13.clone.1 | convolution fusion | flops 3273129984 | bytes 110198784 | tf_op jit(solution)/shard_map/while/body/eval_jaxpr/bhqk,bkhe->bqhe/dot_general | solution.py:58
  538.8 15.8 %copy.32 = bf16[16,1024,3,64]{3,0,2,1:T(8,128)(2,1)} copy(bf16[16,1024,3,64]{1,3,2,0:T(8,128)(2,1)} %get-tuple-element.243) | data formatting | bytes 12582912 | tf_op jit(solution)/shard_map/while | solution.py:61
  554.6 13.2 %reshape.148 = bf16[4,2,393216]{2,1,0:T(2,128)(2,1)} reshape(bf16[1024,3,16,64]{3,2,1,0:T(8,128)(2,1)} %bitcast.57) | data formatting | bytes 12582912
  567.8 5.3 all-to-all-start.1
  573.7 69.8 %all-to-all-done.1 = bf16[4,2,393216]{2,1,0:T(2,128)(2,1)} async-done(((bf16[4,2,393216]{2,1,0:T(2,128)(2,1)}), bf16[4,2,393216]{2,1,0:T(2,128)(2,1)}, u32[]{:S(2)}, u32[]{:S(2)}) %all-to-all-start.1) | async-done | bytes 6291488 | tf_op jit(solution)/shard_map/all_to_all | solution.py:79
  643.4 12.6 %reshape.149 = bf16[1024,3,16,64]{3,2,1,0:T(8,128)(2,1)} reshape(bf16[4,2,393216]{2,1,0:T(2,128)(2,1)} %all-to-all-done.1) | data formatting | bytes 12582912
  656.1 14.1 %copy.33 = bf16[16,4,256,3,64]{2,4,3,1,0:T(8,128)(2,1)} copy(bf16[16,4,256,3,64]{4,0,3,2,1:T(8,128)(2,1)} %bitcast.58) | data formatting | bytes 12582912 | tf_op jit(solution)/shard_map/all_to_all | solution.py:79
  670.2 12.2 %fusion.33 = bf16[16,256,768]{2,1,0:T(8,128)(2,1)} fusion(f32[768]{0:T(1024)} %convert_element_type.73, bf16[16,256,12,64]{1,3,2,0:T(8,128)(2,1)} %bitcast.61, bf16[12,64,768,1]{2,1,0,3:T(8,128)(2,1)} %bitcast.64, f32[768]{0:T(1024)} %convert_element_type.65, f32[768]{0:T(1024)} %convert_element_type.64, f32[16,256]{1,0:T(8,128)} %add_rsqrt_fusion, ...), kind=kOutput, calls=%fused_computation.38 | convolution fusion | flops 4866441216 | bytes 20096000 | tf_op jit(solution)/shard_map/bshe,hef->bsf/dot_general | solution.py:81
  (42 shorter events, 3.3 us)
Async XLA Ops:
  0.6 11.5 %copy-start = (bf16[768,12,3,64]{0,3,2,1:T(8,128)(2,1)S(1)}, bf16[768,12,3,64]{0,3,2,1:T(8,128)(2,1)}, u32[]{:S(2)}) copy-start(bf16[768,12,3,64]{0,3,2,1:T(8,128)(2,1)} %param.18) | copy-start | bytes 10616836
  0.6 9.6 %copy-start.9 = (bf16[768]{0:T(1024)(128)(2,1)S(1)}, bf16[768]{0:T(1024)(128)(2,1)}, u32[]{:S(2)}) copy-start(bf16[768]{0:T(1024)(128)(2,1)} %param.16) | copy-start | bytes 4612
  0.7 10.2 %copy-start.10 = (bf16[768]{0:T(1024)(128)(2,1)S(1)}, bf16[768]{0:T(1024)(128)(2,1)}, u32[]{:S(2)}) copy-start(bf16[768]{0:T(1024)(128)(2,1)} %param.17) | copy-start | bytes 4612
  0.7 10.8 %copy-start.8 = (bf16[12,3,64]{2,1,0:T(4,128)(2,1)S(1)}, bf16[12,3,64]{2,1,0:T(4,128)(2,1)}, u32[]{:S(2)}) copy-start(bf16[12,3,64]{2,1,0:T(4,128)(2,1)} %param.19) | copy-start | bytes 13828
  4.9 28.6 %copy-start.2 = (f32[16,256]{1,0:T(8,128)}, f32[16,256]{1,0:T(8,128)S(1)}, u32[]{:S(2)}) copy-start(f32[16,256]{1,0:T(8,128)S(1)} %broadcast_multiply_fusion) | copy-start | bytes 49156
  33.5 4.6 slice-start
  38.1 9.1 %copy-start.4 = (s32[16,256]{1,0:T(8,128)S(1)}, s32[16,256]{1,0:T(8,128)}, u32[]{:S(2)}) copy-start(s32[16,256]{1,0:T(8,128)} %param.14) | copy-start | bytes 49156
  38.1 9.1 %copy-start.5 = (s32[16,256]{1,0:T(8,128)S(1)}, s32[16,256]{1,0:T(8,128)}, u32[]{:S(2)}) copy-start(s32[16,256]{1,0:T(8,128)} %param.13) | copy-start | bytes 49156
  38.1 9.2 %copy-start.12 = (f32[16]{0:T(128)S(1)}, f32[16]{0:T(128)}, u32[]{:S(2)}) copy-start(f32[16]{0:T(128)} %multiply_power_fusion) | copy-start | bytes 196
  73.6 213.4 %all-to-all-start = ((bf16[16,256,12,3,64]{1,4,3,0,2:T(8,128)(2,1)}), bf16[16,256,12,3,64]{1,4,3,0,2:T(8,128)(2,1)}, u32[]{:S(2)}, u32[]{:S(2)}) async-start(bf16[16,256,12,3,64]{1,4,3,0,2:T(8,128)(2,1)} %pad_maximum_fusion), calls=%async_computation | async-start | bytes 37748736 | tf_op jit(solution)/shard_map/all_to_all | solution.py:75
  342.5 18.9 %copy-start.6 = (s32[16]{0:T(128)S(1)}, s32[16]{0:T(128)}, u32[]{:S(2)}) copy-start(s32[16]{0:T(128)} %param.15) | copy-start | bytes 196
  413.7 36.2 %copy-start.7 = (s32[16]{0:T(128)S(1)}, s32[16]{0:T(128)}, u32[]{:S(2)}) copy-start(s32[16]{0:T(128)} %get-tuple-element.252) | copy-start | bytes 196 | tf_op jit(solution)/shard_map/while
  502.6 36.2 %copy-start.7 = (s32[16]{0:T(128)S(1)}, s32[16]{0:T(128)}, u32[]{:S(2)}) copy-start(s32[16]{0:T(128)} %get-tuple-element.252) | copy-start | bytes 196 | tf_op jit(solution)/shard_map/while
  554.6 18.5 %copy-start.11 = (bf16[768]{0:T(1024)(128)(2,1)S(1)}, bf16[768]{0:T(1024)(128)(2,1)}, u32[]{:S(2)}) copy-start(bf16[768]{0:T(1024)(128)(2,1)} %param.21) | copy-start | bytes 4612
  567.8 75.6 %all-to-all-start.1 = ((bf16[4,2,393216]{2,1,0:T(2,128)(2,1)}), bf16[4,2,393216]{2,1,0:T(2,128)(2,1)}, u32[]{:S(2)}, u32[]{:S(2)}) async-start(bf16[4,2,393216]{2,1,0:T(2,128)(2,1)} %reshape.148), calls=%async_computation.1 | async-start | bytes 12582912 | tf_op jit(solution)/shard_map/all_to_all | solution.py:79
  656.1 14.1 %copy-start.3 = (f32[16,256]{1,0:T(8,128)S(1)}, f32[16,256]{1,0:T(8,128)}, u32[]{:S(2)}) copy-start(f32[16,256]{1,0:T(8,128)} %copy-done.2) | copy-start | bytes 49156
  670.2 12.3 %copy-start.1 = (bf16[768,12,3,64]{0,3,2,1:T(8,128)(2,1)S(1)}, bf16[768,12,3,64]{0,3,2,1:T(8,128)(2,1)}, u32[]{:S(2)}) copy-start(bf16[768,12,3,64]{0,3,2,1:T(8,128)(2,1)} %param.18) | copy-start | bytes 10616836
where the time goes:
time: 688 us; the launch traced here: 683 us
  waiting for transfers between devices  276 us (40%)
  matrix products  194 us (28%)
  local copies, waits for them, and re-layouts  137 us (20%)
  other arithmetic  62.4 us (9%)
  starting transfers between devices  12.6 us (2%)
    all_to_all x1, waiting for transfers between devices, local_block(): by_heads = lax.all_to_all(qkv_rot, 'sp', 2, 1, tiled=True)  206 us
    sub x2, matrix products, attend_block(): jax.nn.softmax(jnp.where(visible, scores, -jnp.inf), axis=-1)  88.1 us
    dot_general x2, matrix products, attend_block(): jnp.einsum('bhqk,bkhe->bqhe', attn_probs, value_heads, preferred_element_...  72.4 us
    all_to_all x1, waiting for transfers between devices, local_block(): by_tokens = lax.all_to_all(context, 'sp', 1, 2, tiled=True)  69.8 us
    all_to_all x2, local copies, waits for them, and re-layouts, local_block(): by_heads = lax.all_to_all(qkv_rot, 'sp', 2, 1, tiled=True)  55.4 us
    unnamed x26, local copies, waits for them, and re-layouts  25.9 us
    dot_general x1, matrix products, local_block(): jnp.einsum('bsd,dhte->bshte', normed, w_qkv, preferred_element_type=jnp.f...  21.4 us
    or x4, other arithmetic, attend_block(): ctx_visible | (key_pos[None, None, None, :] <= q_pos[None, None, :, None])  16 us
  transfers between devices with their start and end apart: 2, of which 2 were waited for; matrix products, arithmetic and copies ran while one was open for 0% of the time, Pallas kernels for 0%

commit v1 on v0

v1 whole, which is shorter than its diff:
```python
import functools
import math

import jax
import jax.numpy as jnp
import numpy as np
from jax import lax
from jax.experimental import pallas as pl
from jax.experimental.pallas import tpu as pltpu
from jax.sharding import PartitionSpec as P

ALPHA = math.sqrt(56.0)
ROPE_BASE = 10000.0
LN_EPS = 1e-5
MESH = pl.DeviceIdType.MESH
F32 = jnp.float32
BF16 = jnp.bfloat16

ROWS = 16
PART = 256
SEQ = 1024
HID = 768
HEAD = 64
CHIP = 512
LOCAL = 6
WIDE = LOCAL * HEAD
EXP_SCALE = math.log2(math.e) / math.sqrt(HEAD)
CHUNK = 64


def rope_tables():
    freq = ROPE_BASE ** (-np.arange(0, 32, 2).astype(np.float64) / 32.0)
    angle = freq.astype(np.float32)[:, None] * np.arange(SEQ, dtype=np.float32)[None, :]
    return np.cos(angle.astype(np.float64)).astype(np.float32), np.sin(angle.astype(np.float64)).astype(np.float32)


def nt_dot(a, b):
    return lax.dot_general(a, b, (((1,), (1,)), ((), ())), preferred_element_type=F32)


def kernel(hid_hbm, pos_ref, ctx_ref, gamma_ref, beta_ref, bd_ref, w_hbm, bias_hbm, wd_hbm, tcos_ref, tsin_ref,
           out_ref, ko_ref, vo_ref,
           a_all, posr, w_sc, b_sc, wd_sc, y_sc, kt, vt, kk, qbd, ctab, stab, s_0, s_1, s_2, s_3, p_0, p_1, p_2, p_3, top_sc, inv_sc, ctx_buf, ctx_recv,
           hid_sem, w_sem, xs_sem, xr_sem, ds_sem, dr_sem, rs_sem, rr_sem, cs_sem, cr_sem, ps_sem, pr_sem):
    step = pl.program_id(0)
    s_refs, p_refs = (s_0, s_1, s_2, s_3), (p_0, p_1, p_2, p_3)
    me = lax.axis_index('sp')
    core = lax.rem(me, 2)
    chip = me // 2
    other = 1 - chip
    peer_x = other * 2 + core
    peer_d = chip * 2 + 1 - core
    peer_xd = other * 2 + 1 - core

    def send_x(r):
        return pltpu.make_async_remote_copy(a_all.at[r, me], a_all.at[r, me], xs_sem.at[r], xr_sem.at[r], device_id={'sp': peer_x}, device_id_type=MESH)

    def send_d(r):
        return pltpu.make_async_remote_copy(a_all.at[r, me], a_all.at[r, me], ds_sem.at[r], dr_sem.at[r], device_id={'sp': peer_d}, device_id_type=MESH)

    def recv_x(r):
        return pltpu.make_async_remote_copy(a_all.at[r, peer_x], a_all.at[r, peer_x], xs_sem.at[r], xr_sem.at[r], device_id={'sp': peer_x}, device_id_type=MESH)

    def recv_d(r):
        return pltpu.make_async_remote_copy(a_all.at[r, peer_d], a_all.at[r, peer_d], ds_sem.at[r], dr_sem.at[r], device_id={'sp': peer_d}, device_id_type=MESH)

    def relay(r):
        return pltpu.make_async_remote_copy(a_all.at[r, peer_x], a_all.at[r, peer_x], rs_sem.at[r], rr_sem.at[r], device_id={'sp': peer_d}, device_id_type=MESH)

    def recv_relay(r):
        return pltpu.make_async_remote_copy(a_all.at[r, peer_xd], a_all.at[r, peer_xd], rs_sem.at[r], rr_sem.at[r], device_id={'sp': peer_d}, device_id_type=MESH)

    def swap_ctx(r):
        return pltpu.make_async_remote_copy(ctx_buf.at[r, 1 - core], ctx_recv.at[r], cs_sem.at[r], cr_sem.at[r], device_id={'sp': peer_d}, device_id_type=MESH)

    def swap_pos(n, peer):
        return pltpu.make_async_remote_copy(pos_ref.at[:, pl.ds(128, 128)], posr.at[me], ps_sem.at[n], pr_sem.at[n], device_id={'sp': peer}, device_id_type=MESH)

    def recv_pos(n, peer):
        return pltpu.make_async_remote_copy(pos_ref.at[:, pl.ds(128, 128)], posr.at[peer], ps_sem.at[n], pr_sem.at[n], device_id={'sp': peer}, device_id_type=MESH)

    def load_hidden(r):
        return pltpu.make_async_copy(hid_hbm.at[r], a_all.at[r, me], hid_sem.at[r])

    def weight_copies():
        copies = []
        for group, owner in enumerate((me, peer_x)):
            for slot, kind in ((0, 1), (6, 2), (12, 0)):
                for h in range(3):
                    copies.append((w_hbm.at[owner * 3 + h, kind], w_sc.at[slot + 3 * group + h]))
                    copies.append((bias_hbm.at[owner * 3 + h, kind], b_sc.at[slot + 3 * group + h]))
        for slot, owner in enumerate((me, peer_x, peer_d, peer_xd)):
            copies.append((wd_hbm.at[pl.ds(pl.multiple_of(owner * 192, 64), 192)], wd_sc.at[pl.ds(slot * 192, 192)]))
        return [pltpu.make_async_copy(src, dst, w_sem.at[i]) for i, (src, dst) in enumerate(copies)]

    def norm_row(r):
        gamma = gamma_ref[...].astype(F32)
        beta = beta_ref[...].astype(F32)
        for t in range(0, PART, 32):
            wide = a_all[r, me, pl.ds(t, 32), :].astype(F32)
            mean = jnp.sum(wide, axis=-1, keepdims=True) * (1.0 / HID)
            cent = wide - mean
            var = jnp.sum(cent * cent, axis=-1, keepdims=True) * (1.0 / HID)
            a_all[r, me, pl.ds(t, 32), :] = (cent * lax.rsqrt(var + LN_EPS) * gamma + beta).astype(BF16)

    @pl.when(step == 0)
    def _():
        def fetch(r, c):
            load_hidden(r).start()
            return c

        lax.fori_loop(0, ROWS, fetch, 0)
        for c in weight_copies():
            c.start()
        barrier = pltpu.get_barrier_semaphore()
        for peer in (peer_x, peer_d, peer_xd):
            pl.semaphore_signal(barrier, inc=1, device_id={'sp': peer}, device_id_type=MESH)
        pl.semaphore_wait(barrier, 3)
        for n, peer in enumerate((peer_x, peer_d, peer_xd)):
            swap_pos(n, peer).start()
        posr[me] = pos_ref[:, 128:256]
        qbd[...] = jnp.zeros_like(qbd)

        def norm_and_send(r, c):
            load_hidden(r).wait()
            norm_row(r)

            @pl.when(r > 0)
            def _():
                send_x(r - 1).start()
                send_d(r - 1).start()

            return c

        lax.fori_loop(0, ROWS, norm_and_send, 0)
        for c in weight_copies():
            c.wait()
        for n, peer in enumerate((peer_x, peer_d, peer_xd)):
            recv_pos(n, peer).wait()
        send_x(ROWS - 1).start()
        send_d(ROWS - 1).start()

    def build_tables(r):
        tcos = tcos_ref[...]
        tsin = tsin_ref[...]
        lane = lax.broadcasted_iota(jnp.int32, (16, SEQ), 1)
        ctx = ctx_ref[r]
        last = posr[3, pl.ds(r, 1), :]
        last_lane = lax.broadcasted_iota(jnp.int32, (1, 128), 1)
        m_pos = jnp.sum(jnp.where(last_lane == 127, last, 0), axis=1, keepdims=True)

        def pick(table, hit):
            return jnp.sum(jnp.where(hit, table, 0.0), axis=1, keepdims=True)

        at_m = lane == m_pos
        at_c = lane == ctx - 1
        in_ctx = lane < ctx
        cos_c, sin_c = pick(tcos, at_c), pick(tsin, at_c)
        ctab[0:16] = jnp.where(in_ctx, tcos, pick(tcos, at_m))
        stab[0:16] = jnp.where(in_ctx, tsin, pick(tsin, at_m))
        ctab[16:32] = jnp.where(in_ctx, 1.0, tcos * cos_c + tsin * sin_c)
        stab[16:32] = jnp.where(in_ctx, 0.0, tsin * cos_c - tcos * sin_c)

    def project(r, which, with_q):
        rows = 3 * WIDE if with_q else 2 * WIDE
        tokens = a_all[r, pl.ds(2 * which, 2)].reshape(CHIP, HID)
        y_sc[0:rows] = nt_dot(w_sc[0:rows // HEAD].reshape(rows, HID), tokens)
        for lt in range(CHIP // 128):
            cols = pl.ds(pl.multiple_of(which * CHIP + lt * 128, 128), 128)
            ycols = slice(lt * 128, lt * 128 + 128)
            for h in range(LOCAL):
                for half in range(2):
                    cos = ctab[16 * half:16 * half + 16, cols]
                    sin = stab[16 * half:16 * half + 16, cols]

                    def rotated(base):
                        u0 = base + h * HEAD + half * 32
                        b0 = half * 32
                        bias = b_sc.at[base // HEAD + h]
                        u = (y_sc[u0:u0 + 16, ycols] + bias[b0:b0 + 16]).astype(BF16).astype(F32)
                        w = (y_sc[u0 + 16:u0 + 32, ycols] + bias[b0 + 16:b0 + 32]).astype(BF16).astype(F32)
                        return (u * cos - w * sin).astype(BF16), (w * cos + u * sin).astype(BF16)

                    k0 = h * HEAD + half * 32
                    ku, kw = rotated(0)
                    kt[k0:k0 + 16, cols] = ku
                    kt[k0 + 16:k0 + 32, cols] = kw
                    if with_q:
                        qu, qw = rotated(2 * WIDE)
                        q0 = (h % 2) * HEAD + half * 32
                        qc = slice((h % 2) * CHIP + lt * 128, (h % 2) * CHIP + lt * 128 + 128)
                        qbd[h // 2, q0:q0 + 16, qc] = qu
                        qbd[h // 2, q0 + 16:q0 + 32, qc] = qw
                v0 = WIDE + h * HEAD
                vt[h * HEAD:(h + 1) * HEAD, cols] = (y_sc[v0:v0 + HEAD, ycols] + b_sc[6 + h]).astype(BF16)

    def attend(r, this_chip):
        spec = ((768, 256), (768, 256)) if this_chip == 0 else ((768, 512), (1024, 768))

        def score(pair, j):
            for qb in range(2):
                key_len, mask_from = spec[qb]
                q0 = j * CHIP + qb * PART
                scores = jnp.dot(kk[pair, 0:key_len, :], qbd[pair, :, q0:q0 + PART], preferred_element_type=F32)
                q_pos = this_chip * CHIP + qb * PART + lax.broadcasted_iota(jnp.int32, (1, PART), 1)
                limit = jnp.maximum(q_pos, ctx_ref[r] - 1)
                top = None
                for k0 in range(0, key_len, CHUNK):
                    part = scores[k0:k0 + CHUNK]
                    if k0 >= mask_from:
                        k_pos = k0 + lax.broadcasted_iota(jnp.int32, (CHUNK, PART), 0)
                        part = jnp.where(k_pos <= limit, part, -jnp.inf)
                    s_refs[2 * j + qb][k0:k0 + CHUNK] = part
                    peak = jnp.max(part.reshape(CHUNK // 8, 8, PART), axis=0)
                    top = peak if top is None else jnp.maximum(top, peak)
                top_sc[2 * j + qb] = jnp.broadcast_to(jnp.max(top, axis=0, keepdims=True) * EXP_SCALE, (8, PART))

        def weigh(j):
            for qb in range(2):
                key_len = spec[qb][0]
                top = top_sc[2 * j + qb, 0:1]
                total = jnp.zeros((8, PART), F32)
                for k0 in range(0, key_len, CHUNK):
                    prob = jnp.exp2(s_refs[2 * j + qb][k0:k0 + CHUNK] * EXP_SCALE - top)
                    total = total + jnp.sum(prob.reshape(CHUNK // 8, 8, PART), axis=0)
                    p_refs[2 * j + qb][k0:k0 + CHUNK] = prob.astype(BF16)
                inv_sc[2 * j + qb] = jnp.broadcast_to(1.0 / jnp.sum(total, axis=0, keepdims=True), (8, PART))

        def mix(pair, j):
            v_rows = pl.ds(pl.multiple_of((2 * pair + j) * HEAD, HEAD), HEAD)
            for qb in range(2):
                key_len = spec[qb][0]
                mixed = jnp.dot(vt[v_rows, 0:key_len], p_refs[2 * j + qb][0:key_len], preferred_element_type=F32)
                ctx_buf[r, qb, v_rows, :] = (mixed * inv_sc[2 * j + qb, 0:1]).astype(BF16)

        score(0, 0)
        score(0, 1)
        weigh(0)

        def one_pair(pair, c):
            score(pair + 1, 0)
            weigh(1)
            mix(pair, 0)
            score(pair + 1, 1)
            weigh(0)
            mix(pair, 1)
            return c

        lax.fori_loop(0, LOCAL // 2 - 1, one_pair, 0)
        weigh(1)
        mix(LOCAL // 2 - 1, 0)
        mix(LOCAL // 2 - 1, 1)

    def dense(r):
        mixed = jnp.concatenate([ctx_buf[r, core], ctx_recv[r]], axis=0)
        dense_out = lax.dot_general(mixed, wd_sc[...], (((0,), (0,)), ((), ())), preferred_element_type=F32)
        normed = a_all[r, me].astype(F32)
        out_ref[0] = (normed * ALPHA + dense_out + bd_ref[...].astype(F32)).astype(BF16)

    @pl.when(step < ROWS)
    def _():
        build_tables(step)
        recv_d(step).wait_recv()
        project(step, chip, True)

    @pl.when(step > 0)
    def _():
        swap_ctx(step - 1).start()

    @pl.when(step < ROWS)
    def _():
        recv_x(step).wait_recv()
        relay(step).start()

    @pl.when(step > 0)
    def _():
        swap_ctx(step - 1).wait_recv()
        dense(step - 1)

    @pl.when(step < ROWS)
    def _():
        recv_relay(step).wait_recv()
        project(step, other, False)
        ko_ref[0] = kt[0:192].reshape(3, HEAD, SEQ)
        vo_ref[0] = vt[0:192].reshape(3, HEAD, SEQ)
        for pair in range(LOCAL // 2):
            kk[pair] = kt[pair * 128:(pair + 1) * 128, :].T

    @pl.when(jnp.logical_and(step < ROWS, chip == 0))
    def _():
        attend(step, 0)

    @pl.when(jnp.logical_and(step < ROWS, chip == 1))
    def _():
        attend(step, 1)

    @pl.when(step == ROWS)
    def _():
        def drain(r, c):
            send_x(r).wait_send()
            send_d(r).wait_send()
            relay(r).wait_send()
            swap_ctx(r).wait_send()
            return c

        lax.fori_loop(0, ROWS, drain, 0)


def solution(mesh):
    seq_spec = P('dp', 'sp', None)
    row_spec = P('dp', 'sp')
    head_spec = P('dp', None, 'sp', None)
    replicated = P()
    tcos, tsin = rope_tables()

    def local_block(hidden, pos_ids, block_ids, ctx_len, ln_gamma, ln_beta, w_qkv, b_qkv, w_dense, b_dense):
        w_t = jnp.transpose(w_qkv, (1, 2, 3, 0))
        bias = jnp.broadcast_to(b_qkv.astype(F32)[..., None], (12, 3, HEAD, 128))
        anywhere = pl.BlockSpec(memory_space=pl.ANY)

        def whole(shape):
            return pl.BlockSpec(shape, lambda i: (0,) * len(shape))

        out, keys_t, values_t = pl.pallas_call(
            kernel,
            grid=(ROWS + 1,),
            out_shape=(
                jax.ShapeDtypeStruct((ROWS, PART, HID), BF16),
                jax.ShapeDtypeStruct((ROWS, 3, HEAD, SEQ), BF16),
                jax.ShapeDtypeStruct((ROWS, 3, HEAD, SEQ), BF16),
            ),
            in_specs=[
                anywhere, whole((ROWS, PART)), pl.BlockSpec(memory_space=pltpu.SMEM),
                whole((1, HID)), whole((1, HID)), whole((1, HID)),
                anywhere, anywhere, anywhere, whole((16, SEQ)), whole((16, SEQ)),
            ],
            out_specs=(
                pl.BlockSpec((1, PART, HID), lambda i: (jnp.maximum(i - 1, 0), 0, 0)),
                pl.BlockSpec((1, 3, HEAD, SEQ), lambda i: (jnp.minimum(i, ROWS - 1), 0, 0, 0)),
                pl.BlockSpec((1, 3, HEAD, SEQ), lambda i: (jnp.minimum(i, ROWS - 1), 0, 0, 0)),
            ),
            scratch_shapes=[
                pltpu.VMEM((ROWS, 4, PART, HID), BF16),
                pltpu.VMEM((4, ROWS, 128), jnp.int32),
                pltpu.VMEM((18, HEAD, HID), BF16),
                pltpu.VMEM((18, HEAD, 128), F32),
                pltpu.VMEM((HID, HID), BF16),
                pltpu.VMEM((3 * WIDE, CHIP), F32),
                pltpu.VMEM((WIDE, SEQ), BF16),
                pltpu.VMEM((WIDE, SEQ), BF16),
                pltpu.VMEM((3, SEQ, 128), BF16),
                pltpu.VMEM((3, 128, 2 * CHIP), BF16),
                pltpu.VMEM((32, SEQ), F32),
                pltpu.VMEM((32, SEQ), F32),
                *[pltpu.VMEM((SEQ, PART), F32)] * 4,
                *[pltpu.VMEM((SEQ, PART), BF16)] * 4,
                pltpu.VMEM((4, 8, PART), F32),
                pltpu.VMEM((4, 8, PART), F32),
                pltpu.VMEM((ROWS, 2, WIDE, PART), BF16),
                pltpu.VMEM((ROWS, WIDE, PART), BF16),
                pltpu.SemaphoreType.DMA((ROWS,)),
                pltpu.SemaphoreType.DMA((40,)),
            ] + [pltpu.SemaphoreType.DMA((ROWS,))] * 8 + [pltpu.SemaphoreType.DMA((3,))] * 2,
            compiler_params=pltpu.CompilerParams(
                collective_id=0, has_side_effects=True, vmem_limit_bytes=62 * 1024 * 1024, dimension_semantics=('arbitrary',)),
            name='glm_block',
        )(hidden, pos_ids, ctx_len, ln_gamma.reshape(1, HID), ln_beta.reshape(1, HID), b_dense.reshape(1, HID),
          w_t, bias, w_dense, jnp.asarray(tcos), jnp.asarray(tsin))
        return out, jnp.transpose(keys_t, (0, 3, 1, 2)), jnp.transpose(values_t, (0, 3, 1, 2))

    return jax.shard_map(local_block, mesh=mesh, in_specs=(seq_spec, row_spec, row_spec, P('dp'), replicated, replicated, replicated, replicated, replicated, replicated), out_specs=(seq_spec, head_spec, head_spec), check_vma=False)
```

time: 688 us -> 181 us (0.26)
  waiting for transfers between devices: 276 us -> 0 us
  matrix products: 194 us -> 0 us
  Pallas kernels: 0 us -> 157 us
  local copies, waits for them, and re-layouts: 137 us -> 19.7 us
  other arithmetic: 62.4 us -> 0.01 us
  starting transfers between devices: 12.6 us -> 0 us
    all_to_all x2 -> x0, waiting for transfers between devices: 276 us -> none  [the longest x1 206 us: local_block(): by_heads = lax.all_to_all(qkv_rot, 'sp', 2, 1, tiled=True)]
    pallas_call x0 -> x1, Pallas kernels: none -> 157 us  [local_block(): pl.pallas_call(kernel, grid=(ROWS + 1,), out_shape=(jax.ShapeDtypeStruct(...]
    dot_general x4 -> x0, matrix products: 106 us -> none  [the longest x2 72.4 us: attend_block(): jnp.einsum('bhqk,bkhe->bqhe', attn_probs, value_heads, preferred_element_...]
    sub x2 -> x0, matrix products: 88.1 us -> none  [attend_block(): jax.nn.softmax(jnp.where(visible, scores, -jnp.inf), axis=-1)]
    all_to_all x3 -> x0, local copies, waits for them, and re-layouts: 69.6 us -> none  [the longest x2 55.4 us: local_block(): by_heads = lax.all_to_all(qkv_rot, 'sp', 2, 1, tiled=True)]
    or x4 -> x0, other arithmetic: 16 us -> none  [attend_block(): ctx_visible | (key_pos[None, None, None, :] <= q_pos[None, None, :, None])]
    while x5 -> x0, local copies, waits for them, and re-layouts: 15.8 us -> none  [the longest x1 15.8 us: attend(): lax.fori_loop(0, query_len // block_len, attend_block, jnp.zeros_like(que...]
    squeeze x1 -> x0, local copies, waits for them, and re-layouts: 15.4 us -> none  [local_block(): value_heads = by_heads[:, :, :, 2]]
  transfers between devices with their start and end apart: 2 -> 0, of which waited for: 2 -> 0; matrix products, arithmetic and copies ran while one was open for 0% -> 0% of each run, Pallas kernels for 0% -> 0%
where the time goes in v1:
time: 181 us; the launch traced here: 178 us
  Pallas kernels  157 us (87%)
  local copies, waits for them, and re-layouts  19.7 us (11%)
    pallas_call x1, Pallas kernels, local_block(): pl.pallas_call(kernel, grid=(ROWS + 1,), out_shape=(jax.ShapeDtypeStruct(...  157 us
    unnamed x9, local copies, waits for them, and re-layouts  13.8 us

profile of v1, /device:TPU:0, one launch (start us, length us, event | category | flops | bytes accessed | tf_op | source)
XLA Modules:
  0.0 177.7 jit_solution(11521045065649719890)
XLA Ops:
  0.6 1.3 reshape.16.gamma_ref
  1.9 1.3 reshape.17.beta_ref
  3.2 1.3 reshape.18.bd_ref
  4.4 2.1 %broadcast_in_dim.2.bias_hbm = f32[12,3,64,128]{3,2,1,0:T(8,128)} broadcast(bf16[12,3,64]{2,1,0:T(4,128)(2,1)} %param.18), dimensions={0,1,2} | broadcast | bytes 1184256 | tf_op jit(solution)/shard_map/broadcast_in_dim | solution.py:318
  6.5 157.3 %glm_block.1 = (bf16[16,256,768]{2,1,0:T(8,128)(2,1)}, bf16[16,3,64,1024]{3,2,1,0:T(8,128)(2,1)}, bf16[16,3,64,1024]{3,2,1,0:T(8,128)(2,1)}) custom-call(bf16[16,256,768]{2,1,0:T(8,128)(2,1)} %hid_hbm.1, s32[16,256]{1,0:T(8,128)} %pos_ref.1, s32[16]{0:T(128)} %ctx_ref.1, bf16[1,768]{1,0:T(2,128)(2,1)} %reshape.16.gamma_ref, ...), custom_call_target="tpu_custom_call" | custom-call | tf_op jit(solution)/shard_map/glm_block/pallas_call | solution.py:324
  163.8 0.0 copy-start
  163.8 0.0 slice-start
  163.8 6.7 %copy.17 = bf16[16,256,768]{2,1,0:T(8,128)(2,1)} copy(bf16[16,256,768]{2,1,0:T(8,128)(2,1)} %get-tuple-element.12) | data formatting | bytes 12582912
  170.5 0.0 copy-done
  170.5 0.0 slice-start.1
  170.5 3.2 %copy.18 = bf16[16,1024,3,64]{1,3,2,0:T(8,128)(2,1)} copy(bf16[16,1024,3,64]{1,3,2,0:T(8,128)(2,1)S(1)} %bitcast.6) | data formatting | bytes 12582912
  173.7 0.0 slice-done
  173.7 1.2 slice-done.1
  175.0 2.7 %copy.19 = bf16[16,1024,3,64]{1,3,2,0:T(8,128)(2,1)} copy(bf16[16,1024,3,64]{1,3,2,0:T(8,128)(2,1)S(1)} %bitcast.5) | data formatting | bytes 12582912
  (1 shorter events, 0.0 us)
Async XLA Ops:
  163.8 6.7 %copy-start = (bf16[16,3,64,1024]{3,2,1,0:T(8,128)(2,1)S(1)}, bf16[16,3,64,1024]{3,2,1,0:T(8,128)(2,1)}, u32[]{:S(2)}) copy-start(bf16[16,3,64,1024]{3,2,1,0:T(8,128)(2,1)} %get-tuple-element.7) | copy-start | bytes 18874372
  163.8 9.9 %slice-start = ((s8[6291456]{0:T(1024)(128)(4,1)}), s8[4194304]{0:T(1024)(128)(4,1)S(1)}, s32[]{:S(2)}) async-start(s8[6291456]{0:T(1024)(128)(4,1)} %bitcast.3), calls=%async_computation | async-start | bytes 8388608
  170.5 4.4 %slice-start.1 = ((s8[6291456]{0:T(1024)(128)(4,1)}), s8[2097152]{0:T(1024)(128)(4,1)S(1)}, s32[]{:S(2)}) async-start(s8[6291456]{0:T(1024)(128)(4,1)} %bitcast.3), calls=%async_computation.1 | async-start | bytes 4194304

commit v2 on v1

--- a/solution.py
+++ b/solution.py
@@ -38,7 +38,7 @@
     return lax.dot_general(a, b, (((1,), (1,)), ((), ())), preferred_element_type=F32)
 
 
-def kernel(hid_hbm, pos_ref, ctx_ref, gamma_ref, beta_ref, bd_ref, w_hbm, bias_hbm, wd_hbm, tcos_ref, tsin_ref,
+def kernel(hid_hbm, pos_ref, ctx_ref, gamma_ref, beta_ref, bd_ref, w_hbm, bias_ref, wd_hbm, tcos_ref, tsin_ref,
            out_ref, ko_ref, vo_ref,
            a_all, posr, w_sc, b_sc, wd_sc, y_sc, kt, vt, kk, qbd, ctab, stab, s_0, s_1, s_2, s_3, p_0, p_1, p_2, p_3, top_sc, inv_sc, ctx_buf, ctx_recv,
            hid_sem, w_sem, xs_sem, xr_sem, ds_sem, dr_sem, rs_sem, rr_sem, cs_sem, cr_sem, ps_sem, pr_sem):
@@ -88,20 +88,26 @@
             for slot, kind in ((0, 1), (6, 2), (12, 0)):
                 for h in range(3):
                     copies.append((w_hbm.at[owner * 3 + h, kind], w_sc.at[slot + 3 * group + h]))
-                    copies.append((bias_hbm.at[owner * 3 + h, kind], b_sc.at[slot + 3 * group + h]))
         for slot, owner in enumerate((me, peer_x, peer_d, peer_xd)):
             copies.append((wd_hbm.at[pl.ds(pl.multiple_of(owner * 192, 64), 192)], wd_sc.at[pl.ds(slot * 192, 192)]))
         return [pltpu.make_async_copy(src, dst, w_sem.at[i]) for i, (src, dst) in enumerate(copies)]
 
     def norm_row(r):
-        gamma = gamma_ref[...].astype(F32)
-        beta = beta_ref[...].astype(F32)
+        gamma = gamma_ref[...].astype(F32).reshape(1, HID)
+        beta = beta_ref[...].astype(F32).reshape(1, HID)
         for t in range(0, PART, 32):
             wide = a_all[r, me, pl.ds(t, 32), :].astype(F32)
             mean = jnp.sum(wide, axis=-1, keepdims=True) * (1.0 / HID)
             cent = wide - mean
             var = jnp.sum(cent * cent, axis=-1, keepdims=True) * (1.0 / HID)
             a_all[r, me, pl.ds(t, 32), :] = (cent * lax.rsqrt(var + LN_EPS) * gamma + beta).astype(BF16)
+
+    def spread_bias():
+        for group, owner in enumerate((me, peer_x)):
+            for slot, kind in ((0, 1), (6, 2), (12, 0)):
+                for h in range(3):
+                    row = bias_ref[owner * 3 + h, kind:kind + 1, :].astype(F32)
+                    b_sc[slot + 3 * group + h] = jnp.broadcast_to(row, (128, HEAD)).T
 
     @pl.when(step == 0)
     def _():
@@ -120,6 +126,7 @@
             swap_pos(n, peer).start()
         posr[me] = pos_ref[:, 128:256]
         qbd[...] = jnp.zeros_like(qbd)
+        spread_bias()
 
         def norm_and_send(r, c):
             load_hidden(r).wait()
@@ -255,22 +262,19 @@
         mixed = jnp.concatenate([ctx_buf[r, core], ctx_recv[r]], axis=0)
         dense_out = lax.dot_general(mixed, wd_sc[...], (((0,), (0,)), ((), ())), preferred_element_type=F32)
         normed = a_all[r, me].astype(F32)
-        out_ref[0] = (normed * ALPHA + dense_out + bd_ref[...].astype(F32)).astype(BF16)
+        out_ref[0] = (normed * ALPHA + dense_out + bd_ref[...].astype(F32).reshape(1, HID)).astype(BF16)
+
+    @pl.when(step > 0)
+    def _():
+        swap_ctx(step - 1).start()
 
     @pl.when(step < ROWS)
     def _():
+        recv_x(step).wait_recv()
+        relay(step).start()
         build_tables(step)
         recv_d(step).wait_recv()
         project(step, chip, True)
-
-    @pl.when(step > 0)
-    def _():
-        swap_ctx(step - 1).start()
-
-    @pl.when(step < ROWS)
-    def _():
-        recv_x(step).wait_recv()
-        relay(step).start()
 
     @pl.when(step > 0)
     def _():
@@ -315,7 +319,6 @@
 
     def local_block(hidden, pos_ids, block_ids, ctx_len, ln_gamma, ln_beta, w_qkv, b_qkv, w_dense, b_dense):
         w_t = jnp.transpose(w_qkv, (1, 2, 3, 0))
-        bias = jnp.broadcast_to(b_qkv.astype(F32)[..., None], (12, 3, HEAD, 128))
         anywhere = pl.BlockSpec(memory_space=pl.ANY)
 
         def whole(shape):
@@ -331,8 +334,8 @@
             ),
             in_specs=[
                 anywhere, whole((ROWS, PART)), pl.BlockSpec(memory_space=pltpu.SMEM),
-                whole((1, HID)), whole((1, HID)), whole((1, HID)),
-                anywhere, anywhere, anywhere, whole((16, SEQ)), whole((16, SEQ)),
+                whole((HID,)), whole((HID,)), whole((HID,)),
+                anywhere, whole((12, 3, HEAD)), anywhere, whole((16, SEQ)), whole((16, SEQ)),
             ],
             out_specs=(
                 pl.BlockSpec((1, PART, HID), lambda i: (jnp.maximum(i - 1, 0), 0, 0)),
@@ -359,13 +362,13 @@
                 pltpu.VMEM((ROWS, 2, WIDE, PART), BF16),
                 pltpu.VMEM((ROWS, WIDE, PART), BF16),
                 pltpu.SemaphoreType.DMA((ROWS,)),
-                pltpu.SemaphoreType.DMA((40,)),
+                pltpu.SemaphoreType.DMA((22,)),
             ] + [pltpu.SemaphoreType.DMA((ROWS,))] * 8 + [pltpu.SemaphoreType.DMA((3,))] * 2,
             compiler_params=pltpu.CompilerParams(
                 collective_id=0, has_side_effects=True, vmem_limit_bytes=62 * 1024 * 1024, dimension_semantics=('arbitrary',)),
             name='glm_block',
-        )(hidden, pos_ids, ctx_len, ln_gamma.reshape(1, HID), ln_beta.reshape(1, HID), b_dense.reshape(1, HID),
-          w_t, bias, w_dense, jnp.asarray(tcos), jnp.asarray(tsin))
+        )(hidden, pos_ids, ctx_len, ln_gamma, ln_beta, b_dense,
+          w_t, b_qkv, w_dense, jnp.asarray(tcos), jnp.asarray(tsin))
         return out, jnp.transpose(keys_t, (0, 3, 1, 2)), jnp.transpose(values_t, (0, 3, 1, 2))
 
     return jax.shard_map(local_block, mesh=mesh, in_specs=(seq_spec, row_spec, row_spec, P('dp'), replicated, replicated, replicated, replicated, replicated, replicated), out_specs=(seq_spec, head_spec, head_spec), check_vma=False)

time: 181 us -> 168 us (0.928); the launches traced: 178 us -> 167 us
  local copies, waits for them, and re-layouts: 19.7 us -> 13.8 us
  Pallas kernels: 157 us -> 153 us
    pallas_call x1, Pallas kernels: 157 us -> 153 us  [local_block(): pl.pallas_call(kernel, grid=(ROWS + 1,), out_shape=(jax.ShapeDtypeStruct(...]
    reshape x3 -> x0, local copies, waits for them, and re-layouts: 3.8 us -> none  [the longest x1 1.27 us: local_block(): b_dense.reshape(1, HID)]
    broadcast_in_dim x1 -> x0, local copies, waits for them, and re-layouts: 2.09 us -> none  [local_block(): bias = jnp.broadcast_to(b_qkv.astype(F32)[..., None], (12, 3, HEAD, 128))]
where the time goes in v2:
time: 168 us; the launch traced here: 167 us
  Pallas kernels  153 us (91%)
  local copies, waits for them, and re-layouts  13.8 us (8%)
    pallas_call x1, Pallas kernels, local_block(): pl.pallas_call(kernel, grid=(ROWS + 1,), out_shape=(jax.ShapeDtypeStruct(...  153 us
    unnamed x9, local copies, waits for them, and re-layouts  13.8 us

profile of v2, /device:TPU:0, one launch (start us, length us, event | category | flops | bytes accessed | tf_op | source)
XLA Modules:
  0.0 167.3 jit_solution(12184927231543249809)
XLA Ops:
  0.6 152.8 %glm_block.1 = (bf16[16,256,768]{2,1,0:T(8,128)(2,1)}, bf16[16,3,64,1024]{3,2,1,0:T(8,128)(2,1)}, bf16[16,3,64,1024]{3,2,1,0:T(8,128)(2,1)}) custom-call(bf16[16,256,768]{2,1,0:T(8,128)(2,1)} %hid_hbm.1, s32[16,256]{1,0:T(8,128)} %pos_ref.1, s32[16]{0:T(128)} %ctx_ref.1, bf16[768]{0:T(1024)(128)(2,1)} %gamma_ref.1, bf16[768]{0:T(1024)(128)(2,1)} %beta_ref.1, ...), custom_call_target="tpu_custom_call" | custom-call | tf_op jit(solution)/shard_map/glm_block/pallas_call | solution.py:327
  153.5 0.0 copy-start
  153.5 0.0 slice-start
  153.5 6.7 %copy.17 = bf16[16,256,768]{2,1,0:T(8,128)(2,1)} copy(bf16[16,256,768]{2,1,0:T(8,128)(2,1)} %get-tuple-element.12) | data formatting | bytes 12582912
  160.2 0.0 copy-done
  160.2 0.0 slice-start.1
  160.2 3.2 %copy.18 = bf16[16,1024,3,64]{1,3,2,0:T(8,128)(2,1)} copy(bf16[16,1024,3,64]{1,3,2,0:T(8,128)(2,1)S(1)} %bitcast.6) | data formatting | bytes 12582912
  163.4 0.0 slice-done
  163.4 1.2 slice-done.1
  164.6 2.7 %copy.19 = bf16[16,1024,3,64]{1,3,2,0:T(8,128)(2,1)} copy(bf16[16,1024,3,64]{1,3,2,0:T(8,128)(2,1)S(1)} %bitcast.5) | data formatting | bytes 12582912
  (1 shorter events, 0.0 us)
Async XLA Ops:
  153.5 6.7 %copy-start = (bf16[16,3,64,1024]{3,2,1,0:T(8,128)(2,1)S(1)}, bf16[16,3,64,1024]{3,2,1,0:T(8,128)(2,1)}, u32[]{:S(2)}) copy-start(bf16[16,3,64,1024]{3,2,1,0:T(8,128)(2,1)} %get-tuple-element.7) | copy-start | bytes 18874372
  153.5 9.9 %slice-start = ((s8[6291456]{0:T(1024)(128)(4,1)}), s8[4194304]{0:T(1024)(128)(4,1)S(1)}, s32[]{:S(2)}) async-start(s8[6291456]{0:T(1024)(128)(4,1)} %bitcast.3), calls=%async_computation | async-start | bytes 8388608
  160.2 4.4 %slice-start.1 = ((s8[6291456]{0:T(1024)(128)(4,1)}), s8[2097152]{0:T(1024)(128)(4,1)S(1)}, s32[]{:S(2)}) async-start(s8[6291456]{0:T(1024)(128)(4,1)} %bitcast.3), calls=%async_computation.1 | async-start | bytes 4194304

commit v3 on v2

--- a/solution.py
+++ b/solution.py
@@ -40,7 +40,7 @@
 
 def kernel(hid_hbm, pos_ref, ctx_ref, gamma_ref, beta_ref, bd_ref, w_hbm, bias_ref, wd_hbm, tcos_ref, tsin_ref,
            out_ref, ko_ref, vo_ref,
-           a_all, posr, w_sc, b_sc, wd_sc, y_sc, kt, vt, kk, qbd, ctab, stab, s_0, s_1, s_2, s_3, p_0, p_1, p_2, p_3, top_sc, inv_sc, ctx_buf, ctx_recv,
+           own, xbuf, dbuf, rbuf, posr, w_sc, b_sc, wd_sc, y_0, y_1, kt, vt, kk, qbd, ctab, stab, s_0, s_1, s_2, s_3, p_0, p_1, p_2, p_3, top_sc, inv_sc, ctx_buf, ctx_recv,
            hid_sem, w_sem, xs_sem, xr_sem, ds_sem, dr_sem, rs_sem, rr_sem, cs_sem, cr_sem, ps_sem, pr_sem):
     step = pl.program_id(0)
     s_refs, p_refs = (s_0, s_1, s_2, s_3), (p_0, p_1, p_2, p_3)
@@ -52,35 +52,29 @@
     peer_d = chip * 2 + 1 - core
     peer_xd = other * 2 + 1 - core
 
+    def remote(src, dst, send_sem, recv_sem, peer):
+        return pltpu.make_async_remote_copy(src, dst, send_sem, recv_sem, device_id={'sp': peer}, device_id_type=MESH)
+
     def send_x(r):
-        return pltpu.make_async_remote_copy(a_all.at[r, me], a_all.at[r, me], xs_sem.at[r], xr_sem.at[r], device_id={'sp': peer_x}, device_id_type=MESH)
+        return remote(own.at[r], xbuf.at[r], xs_sem.at[r], xr_sem.at[r], peer_x)
 
     def send_d(r):
-        return pltpu.make_async_remote_copy(a_all.at[r, me], a_all.at[r, me], ds_sem.at[r], dr_sem.at[r], device_id={'sp': peer_d}, device_id_type=MESH)
-
-    def recv_x(r):
-        return pltpu.make_async_remote_copy(a_all.at[r, peer_x], a_all.at[r, peer_x], xs_sem.at[r], xr_sem.at[r], device_id={'sp': peer_x}, device_id_type=MESH)
-
-    def recv_d(r):
-        return pltpu.make_async_remote_copy(a_all.at[r, peer_d], a_all.at[r, peer_d], ds_sem.at[r], dr_sem.at[r], device_id={'sp': peer_d}, device_id_type=MESH)
+        return remote(own.at[r], dbuf.at[lax.rem(r, 2)], ds_sem.at[r], dr_sem.at[r], peer_d)
 
     def relay(r):
-        return pltpu.make_async_remote_copy(a_all.at[r, peer_x], a_all.at[r, peer_x], rs_sem.at[r], rr_sem.at[r], device_id={'sp': peer_d}, device_id_type=MESH)
-
-    def recv_relay(r):
-        return pltpu.make_async_remote_copy(a_all.at[r, peer_xd], a_all.at[r, peer_xd], rs_sem.at[r], rr_sem.at[r], device_id={'sp': peer_d}, device_id_type=MESH)
+        return remote(xbuf.at[r], rbuf.at[lax.rem(r, 2)], rs_sem.at[r], rr_sem.at[r], peer_d)
 
     def swap_ctx(r):
-        return pltpu.make_async_remote_copy(ctx_buf.at[r, 1 - core], ctx_recv.at[r], cs_sem.at[r], cr_sem.at[r], device_id={'sp': peer_d}, device_id_type=MESH)
+        return remote(ctx_buf.at[lax.rem(r, 2), 1 - core], ctx_recv.at[lax.rem(r, 2)], cs_sem.at[r], cr_sem.at[r], peer_d)
 
     def swap_pos(n, peer):
-        return pltpu.make_async_remote_copy(pos_ref.at[:, pl.ds(128, 128)], posr.at[me], ps_sem.at[n], pr_sem.at[n], device_id={'sp': peer}, device_id_type=MESH)
+        return remote(pos_ref.at[:, pl.ds(128, 128)], posr.at[me], ps_sem.at[n], pr_sem.at[n], peer)
 
     def recv_pos(n, peer):
-        return pltpu.make_async_remote_copy(pos_ref.at[:, pl.ds(128, 128)], posr.at[peer], ps_sem.at[n], pr_sem.at[n], device_id={'sp': peer}, device_id_type=MESH)
+        return remote(pos_ref.at[:, pl.ds(128, 128)], posr.at[peer], ps_sem.at[n], pr_sem.at[n], peer)
 
     def load_hidden(r):
-        return pltpu.make_async_copy(hid_hbm.at[r], a_all.at[r, me], hid_sem.at[r])
+        return pltpu.make_async_copy(hid_hbm.at[r], own.at[r], hid_sem.at[r])
 
     def weight_copies():
         copies = []
@@ -96,11 +90,11 @@
         gamma = gamma_ref[...].astype(F32).reshape(1, HID)
         beta = beta_ref[...].astype(F32).reshape(1, HID)
         for t in range(0, PART, 32):
-            wide = a_all[r, me, pl.ds(t, 32), :].astype(F32)
+            wide = own[r, pl.ds(t, 32), :].astype(F32)
             mean = jnp.sum(wide, axis=-1, keepdims=True) * (1.0 / HID)
             cent = wide - mean
             var = jnp.sum(cent * cent, axis=-1, keepdims=True) * (1.0 / HID)
-            a_all[r, me, pl.ds(t, 32), :] = (cent * lax.rsqrt(var + LN_EPS) * gamma + beta).astype(BF16)
+            own[r, pl.ds(t, 32), :] = (cent * lax.rsqrt(var + LN_EPS) * gamma + beta).astype(BF16)
 
     def spread_bias():
         for group, owner in enumerate((me, peer_x)):
@@ -125,8 +119,6 @@
         for n, peer in enumerate((peer_x, peer_d, peer_xd)):
             swap_pos(n, peer).start()
         posr[me] = pos_ref[:, 128:256]
-        qbd[...] = jnp.zeros_like(qbd)
-        spread_bias()
 
         def norm_and_send(r, c):
             load_hidden(r).wait()
@@ -135,17 +127,18 @@
             @pl.when(r > 0)
             def _():
                 send_x(r - 1).start()
-                send_d(r - 1).start()
 
             return c
 
         lax.fori_loop(0, ROWS, norm_and_send, 0)
+        send_d(0).start()
+        qbd[...] = jnp.zeros_like(qbd)
+        spread_bias()
         for c in weight_copies():
             c.wait()
         for n, peer in enumerate((peer_x, peer_d, peer_xd)):
             recv_pos(n, peer).wait()
         send_x(ROWS - 1).start()
-        send_d(ROWS - 1).start()
 
     def build_tables(r):
         tcos = tcos_ref[...]
@@ -168,12 +161,12 @@
         ctab[16:32] = jnp.where(in_ctx, 1.0, tcos * cos_c + tsin * sin_c)
         stab[16:32] = jnp.where(in_ctx, 0.0, tsin * cos_c - tcos * sin_c)
 
-    def project(r, which, with_q):
-        rows = 3 * WIDE if with_q else 2 * WIDE
-        tokens = a_all[r, pl.ds(2 * which, 2)].reshape(CHIP, HID)
-        y_sc[0:rows] = nt_dot(w_sc[0:rows // HEAD].reshape(rows, HID), tokens)
-        for lt in range(CHIP // 128):
-            cols = pl.ds(pl.multiple_of(which * CHIP + lt * 128, 128), 128)
+    def multiply(y_ref, tokens, rows):
+        y_ref[0:rows] = nt_dot(w_sc[0:rows // HEAD].reshape(rows, HID), tokens)
+
+    def finish(y_ref, part, with_q):
+        for lt in range(PART // 128):
+            cols = pl.ds(pl.multiple_of(part * PART + lt * 128, 128), 128)
             ycols = slice(lt * 128, lt * 128 + 128)
             for h in range(LOCAL):
                 for half in range(2):
@@ -184,8 +177,8 @@
                         u0 = base + h * HEAD + half * 32
                         b0 = half * 32
                         bias = b_sc.at[base // HEAD + h]
-                        u = (y_sc[u0:u0 + 16, ycols] + bias[b0:b0 + 16]).astype(BF16).astype(F32)
-                        w = (y_sc[u0 + 16:u0 + 32, ycols] + bias[b0 + 16:b0 + 32]).astype(BF16).astype(F32)
+                        u = (y_ref[u0:u0 + 16, ycols] + bias[b0:b0 + 16]).astype(BF16).astype(F32)
+                        w = (y_ref[u0 + 16:u0 + 32, ycols] + bias[b0 + 16:b0 + 32]).astype(BF16).astype(F32)
                         return (u * cos - w * sin).astype(BF16), (w * cos + u * sin).astype(BF16)
 
                     k0 = h * HEAD + half * 32
@@ -195,11 +188,18 @@
                     if with_q:
                         qu, qw = rotated(2 * WIDE)
                         q0 = (h % 2) * HEAD + half * 32
-                        qc = slice((h % 2) * CHIP + lt * 128, (h % 2) * CHIP + lt * 128 + 128)
+                        qc = pl.ds(pl.multiple_of((h % 2) * CHIP + lax.rem(part, 2) * PART + lt * 128, 128), 128)
                         qbd[h // 2, q0:q0 + 16, qc] = qu
                         qbd[h // 2, q0 + 16:q0 + 32, qc] = qw
                 v0 = WIDE + h * HEAD
-                vt[h * HEAD:(h + 1) * HEAD, cols] = (y_sc[v0:v0 + HEAD, ycols] + b_sc[6 + h]).astype(BF16)
+                vt[h * HEAD:(h + 1) * HEAD, cols] = (y_ref[v0:v0 + HEAD, ycols] + b_sc[6 + h]).astype(BF16)
+
+    def project(first, first_part, second, second_part, with_q):
+        rows = 3 * WIDE if with_q else 2 * WIDE
+        multiply(y_0, first, rows)
+        multiply(y_1, second, rows)
+        finish(y_0, first_part, with_q)
+        finish(y_1, second_part, with_q)
 
     def attend(r, this_chip):
         spec = ((768, 256), (768, 256)) if this_chip == 0 else ((768, 512), (1024, 768))
@@ -238,7 +238,7 @@
             for qb in range(2):
                 key_len = spec[qb][0]
                 mixed = jnp.dot(vt[v_rows, 0:key_len], p_refs[2 * j + qb][0:key_len], preferred_element_type=F32)
-                ctx_buf[r, qb, v_rows, :] = (mixed * inv_sc[2 * j + qb, 0:1]).astype(BF16)
+                ctx_buf[lax.rem(r, 2), qb, v_rows, :] = (mixed * inv_sc[2 * j + qb, 0:1]).astype(BF16)
 
         score(0, 0)
         score(0, 1)
@@ -259,10 +259,10 @@
         mix(LOCAL // 2 - 1, 1)
 
     def dense(r):
-        mixed = jnp.concatenate([ctx_buf[r, core], ctx_recv[r]], axis=0)
+        mixed = jnp.concatenate([ctx_buf[lax.rem(r, 2), core], ctx_recv[lax.rem(r, 2)]], axis=0)
         dense_out = lax.dot_general(mixed, wd_sc[...], (((0,), (0,)), ((), ())), preferred_element_type=F32)
-        normed = a_all[r, me].astype(F32)
-        out_ref[0] = (normed * ALPHA + dense_out + bd_ref[...].astype(F32).reshape(1, HID)).astype(BF16)
+        normed = own[r].astype(F32)
+        out_ref[r] = (normed * ALPHA + dense_out + bd_ref[...].astype(F32).reshape(1, HID)).astype(BF16)
 
     @pl.when(step > 0)
     def _():
@@ -270,23 +270,30 @@
 
     @pl.when(step < ROWS)
     def _():
-        recv_x(step).wait_recv()
+        send_x(step).wait_recv()
         relay(step).start()
         build_tables(step)
-        recv_d(step).wait_recv()
-        project(step, chip, True)
+        send_d(step).wait_recv()
+        project(own[step], me, dbuf[lax.rem(step, 2)], peer_d, True)
 
     @pl.when(step > 0)
     def _():
-        swap_ctx(step - 1).wait_recv()
+        swap_ctx(step - 1).wait()
         dense(step - 1)
 
     @pl.when(step < ROWS)
     def _():
-        recv_relay(step).wait_recv()
-        project(step, other, False)
-        ko_ref[0] = kt[0:192].reshape(3, HEAD, SEQ)
-        vo_ref[0] = vt[0:192].reshape(3, HEAD, SEQ)
+        relay(step).wait_recv()
+
+    @pl.when(step < ROWS - 1)
+    def _():
+        send_d(step + 1).start()
+
+    @pl.when(step < ROWS)
+    def _():
+        project(xbuf[step], peer_x, rbuf[lax.rem(step, 2)], peer_xd, False)
+        ko_ref[step] = kt[0:192].reshape(3, HEAD, SEQ)
+        vo_ref[step] = vt[0:192].reshape(3, HEAD, SEQ)
         for pair in range(LOCAL // 2):
             kk[pair] = kt[pair * 128:(pair + 1) * 128, :].T
 
@@ -304,10 +311,17 @@
             send_x(r).wait_send()
             send_d(r).wait_send()
             relay(r).wait_send()
-            swap_ctx(r).wait_send()
             return c
 
         lax.fori_loop(0, ROWS, drain, 0)
+
+
+def put(out_vm, keys_vm, values_vm, out_hbm, keys_hbm, values_hbm, sem):
+    copies = [pltpu.make_async_copy(src, dst, sem.at[i]) for i, (src, dst) in enumerate(((out_vm, out_hbm), (keys_vm, keys_hbm), (values_vm, values_hbm)))]
+    for c in copies:
+        c.start()
+    for c in copies:
+        c.wait()
 
 
 def solution(mesh):
@@ -328,27 +342,27 @@
             kernel,
             grid=(ROWS + 1,),
             out_shape=(
-                jax.ShapeDtypeStruct((ROWS, PART, HID), BF16),
-                jax.ShapeDtypeStruct((ROWS, 3, HEAD, SEQ), BF16),
-                jax.ShapeDtypeStruct((ROWS, 3, HEAD, SEQ), BF16),
+                pltpu.VMEM((ROWS, PART, HID), BF16),
+                pltpu.VMEM((ROWS, 3, HEAD, SEQ), BF16),
+                pltpu.VMEM((ROWS, 3, HEAD, SEQ), BF16),
             ),
             in_specs=[
                 anywhere, whole((ROWS, PART)), pl.BlockSpec(memory_space=pltpu.SMEM),
                 whole((HID,)), whole((HID,)), whole((HID,)),
                 anywhere, whole((12, 3, HEAD)), anywhere, whole((16, SEQ)), whole((16, SEQ)),
             ],
-            out_specs=(
-                pl.BlockSpec((1, PART, HID), lambda i: (jnp.maximum(i - 1, 0), 0, 0)),
-                pl.BlockSpec((1, 3, HEAD, SEQ), lambda i: (jnp.minimum(i, ROWS - 1), 0, 0, 0)),
-                pl.BlockSpec((1, 3, HEAD, SEQ), lambda i: (jnp.minimum(i, ROWS - 1), 0, 0, 0)),
-            ),
+            out_specs=(pl.BlockSpec(memory_space=pltpu.VMEM),) * 3,
             scratch_shapes=[
-                pltpu.VMEM((ROWS, 4, PART, HID), BF16),
+                pltpu.VMEM((ROWS, PART, HID), BF16),
+                pltpu.VMEM((ROWS, PART, HID), BF16),
+                pltpu.VMEM((2, PART, HID), BF16),
+                pltpu.VMEM((2, PART, HID), BF16),
                 pltpu.VMEM((4, ROWS, 128), jnp.int32),
                 pltpu.VMEM((18, HEAD, HID), BF16),
                 pltpu.VMEM((18, HEAD, 128), F32),
                 pltpu.VMEM((HID, HID), BF16),
-                pltpu.VMEM((3 * WIDE, CHIP), F32),
+                pltpu.VMEM((3 * WIDE, PART), F32),
+                pltpu.VMEM((3 * WIDE, PART), F32),
                 pltpu.VMEM((WIDE, SEQ), BF16),
                 pltpu.VMEM((WIDE, SEQ), BF16),
                 pltpu.VMEM((3, SEQ, 128), BF16),
@@ -359,16 +373,26 @@
                 *[pltpu.VMEM((SEQ, PART), BF16)] * 4,
                 pltpu.VMEM((4, 8, PART), F32),
                 pltpu.VMEM((4, 8, PART), F32),
-                pltpu.VMEM((ROWS, 2, WIDE, PART), BF16),
-                pltpu.VMEM((ROWS, WIDE, PART), BF16),
+                pltpu.VMEM((2, 2, WIDE, PART), BF16),
+                pltpu.VMEM((2, WIDE, PART), BF16),
                 pltpu.SemaphoreType.DMA((ROWS,)),
                 pltpu.SemaphoreType.DMA((22,)),
             ] + [pltpu.SemaphoreType.DMA((ROWS,))] * 8 + [pltpu.SemaphoreType.DMA((3,))] * 2,
             compiler_params=pltpu.CompilerParams(
-                collective_id=0, has_side_effects=True, vmem_limit_bytes=62 * 1024 * 1024, dimension_semantics=('arbitrary',)),
+                collective_id=0, has_side_effects=True, vmem_limit_bytes=43 * 1024 * 1024, dimension_semantics=('arbitrary',)),
             name='glm_block',
         )(hidden, pos_ids, ctx_len, ln_gamma, ln_beta, b_dense,
           w_t, b_qkv, w_dense, jnp.asarray(tcos), jnp.asarray(tsin))
+        held = [pltpu.with_memory_space_constraint(x, pltpu.VMEM) for x in (out, keys_t, values_t)]
+        out, keys_t, values_t = pl.pallas_call(
+            put,
+            out_shape=[jax.ShapeDtypeStruct(x.shape, BF16) for x in held],
+            in_specs=[pl.BlockSpec(memory_space=pl.ANY)] * 3,
+            out_specs=[anywhere] * 3,
+            scratch_shapes=[pltpu.SemaphoreType.DMA((3,))],
+            compiler_params=pltpu.CompilerParams(vmem_limit_bytes=1024 * 1024),
+            name='put',
+        )(*held)
         return out, jnp.transpose(keys_t, (0, 3, 1, 2)), jnp.transpose(values_t, (0, 3, 1, 2))
 
     return jax.shard_map(local_block, mesh=mesh, in_specs=(seq_spec, row_spec, row_spec, P('dp'), replicated, replicated, replicated, replicated, replicated, replicated), out_specs=(seq_spec, head_spec, head_spec), check_vma=False)

time: 168 us -> 160 us (0.952)
  local copies, waits for them, and re-layouts: 13.8 us -> 0 us
  Pallas kernels: 153 us -> 159 us
    unnamed x9 -> x0, local copies, waits for them, and re-layouts: 13.8 us -> none
    pallas_call x1 -> x2, Pallas kernels: 153 us -> 159 us  [the longest x1 152 us: local_block(): pl.pallas_call(kernel, grid=(ROWS + 1,), out_shape=(pltpu.VMEM((ROWS, PAR...]
where the time goes in v3:
time: 160 us; the launch traced here: 159 us
  Pallas kernels  159 us (99%)
    pallas_call x1, Pallas kernels, local_block(): pl.pallas_call(kernel, grid=(ROWS + 1,), out_shape=(pltpu.VMEM((ROWS, PAR...  152 us
    pallas_call x1, Pallas kernels, local_block(): pl.pallas_call(put, out_shape=[jax.ShapeDtypeStruct(x.shape, BF16) for x...  6.69 us

profile of v3, /device:TPU:0, one launch (start us, length us, event | category | flops | bytes accessed | tf_op | source)
XLA Modules:
  0.0 159.4 jit_solution(3486147148360079287)
XLA Ops:
  0.6 152.1 %glm_block.1 = (bf16[16,256,768]{2,1,0:T(8,128)(2,1)S(1)}, bf16[16,3,64,1024]{3,2,1,0:T(8,128)(2,1)S(1)}, bf16[16,3,64,1024]{3,2,1,0:T(8,128)(2,1)S(1)}) custom-call(bf16[16,256,768]{2,1,0:T(8,128)(2,1)} %hid_hbm.1, s32[16,256]{1,0:T(8,128)} %pos_ref.1, s32[16]{0:T(128)} %ctx_ref.1, bf16[768]{0:T(1024)(128)(2,1)} %gamma_ref.1, bf16[768]{0:T(1024)(128)(2,1)} %beta_ref.1, ...), custom_call_target="tpu_custom_call" | custom-call | tf_op jit(solution)/shard_map/glm_block/pallas_call | solution.py:341
  152.7 6.7 %put.1 = (bf16[16,256,768]{2,1,0:T(8,128)(2,1)}, bf16[16,3,64,1024]{3,2,1,0:T(8,128)(2,1)}, bf16[16,3,64,1024]{3,2,1,0:T(8,128)(2,1)}) custom-call(bf16[16,256,768]{2,1,0:T(8,128)(2,1)S(1)} %get-tuple-element.9.out_vm, bf16[16,3,64,1024]{3,2,1,0:T(8,128)(2,1)S(1)} %get-tuple-element.10.keys_vm, bf16[16,3,64,1024]{3,2,1,0:T(8,128)(2,1)S(1)} %get-tuple-element.11.values_vm), custom_call_target="tpu_custom_call" | custom-call | tf_op jit(solution)/shard_map/put/pallas_call | solution.py:387

commit v4 on v3

--- a/solution.py
+++ b/solution.py
@@ -18,6 +18,7 @@
 
 ROWS = 16
 PART = 256
+HALF = 128
 SEQ = 1024
 HID = 768
 HEAD = 64
@@ -26,6 +27,7 @@
 WIDE = LOCAL * HEAD
 EXP_SCALE = math.log2(math.e) / math.sqrt(HEAD)
 CHUNK = 64
+MIX = 256
 
 
 def rope_tables():
@@ -38,12 +40,12 @@
     return lax.dot_general(a, b, (((1,), (1,)), ((), ())), preferred_element_type=F32)
 
 
-def kernel(hid_hbm, pos_ref, ctx_ref, gamma_ref, beta_ref, bd_ref, w_hbm, bias_ref, wd_hbm, tcos_ref, tsin_ref,
+def kernel(hid_hbm, pos_hbm, ctx_ref, gamma_hbm, beta_hbm, bd_hbm, w_hbm, bias_hbm, wd_hbm, tcos_hbm, tsin_hbm,
            out_ref, ko_ref, vo_ref,
-           own, xbuf, dbuf, rbuf, posr, w_sc, b_sc, wd_sc, y_0, y_1, kt, vt, kk, qbd, ctab, stab, s_0, s_1, s_2, s_3, p_0, p_1, p_2, p_3, top_sc, inv_sc, ctx_buf, ctx_recv,
-           hid_sem, w_sem, xs_sem, xr_sem, ds_sem, dr_sem, rs_sem, rr_sem, cs_sem, cr_sem, ps_sem, pr_sem):
+           pos_ref, gamma_ref, beta_ref, bd_ref, bias_ref, tcos_ref, tsin_ref, own, xbuf, dbuf, rbuf, posr, w_sc, b_sc, wd_sc, y_0, y_1, kt_0, kt_1, kt_2, vt, kk, qbd, ctab, stab, s_0, s_1, s_2, s_3, top_sc, ctx_buf, ctx_recv,
+           t_sem, hid_sem, w_sem, xs_sem, xr_sem, ds_sem, dr_sem, rs_sem, rr_sem, cs_sem, cr_sem, ps_sem, pr_sem):
     step = pl.program_id(0)
-    s_refs, p_refs = (s_0, s_1, s_2, s_3), (p_0, p_1, p_2, p_3)
+    s_refs, kt_refs = (s_0, s_1, s_2, s_3), (kt_0, kt_1, kt_2)
     me = lax.axis_index('sp')
     core = lax.rem(me, 2)
     chip = me // 2
@@ -55,14 +57,19 @@
     def remote(src, dst, send_sem, recv_sem, peer):
         return pltpu.make_async_remote_copy(src, dst, send_sem, recv_sem, device_id={'sp': peer}, device_id_type=MESH)
 
-    def send_x(r):
-        return remote(own.at[r], xbuf.at[r], xs_sem.at[r], xr_sem.at[r], peer_x)
+    def piece(i):
+        return lax.div(i, 2), pl.ds(pl.multiple_of(lax.rem(i, 2) * HALF, HALF), HALF)
+
+    def send_x(i):
+        r, rows = piece(i)
+        return remote(own.at[r, rows], xbuf.at[r, rows], xs_sem.at[i], xr_sem.at[i], peer_x)
 
     def send_d(r):
         return remote(own.at[r], dbuf.at[lax.rem(r, 2)], ds_sem.at[r], dr_sem.at[r], peer_d)
 
-    def relay(r):
-        return remote(xbuf.at[r], rbuf.at[lax.rem(r, 2)], rs_sem.at[r], rr_sem.at[r], peer_d)
+    def relay(i):
+        r, rows = piece(i)
+        return remote(xbuf.at[r, rows], rbuf.at[lax.rem(r, 2), rows], rs_sem.at[i], rr_sem.at[i], peer_d)
 
     def swap_ctx(r):
         return remote(ctx_buf.at[lax.rem(r, 2), 1 - core], ctx_recv.at[lax.rem(r, 2)], cs_sem.at[r], cr_sem.at[r], peer_d)
@@ -75,6 +82,10 @@
 
     def load_hidden(r):
         return pltpu.make_async_copy(hid_hbm.at[r], own.at[r], hid_sem.at[r])
+
+    def small_copies():
+        pairs = ((gamma_hbm, gamma_ref), (beta_hbm, beta_ref), (pos_hbm, pos_ref), (bd_hbm, bd_ref), (bias_hbm, bias_ref), (tcos_hbm, tcos_ref), (tsin_hbm, tsin_ref))
+        return [pltpu.make_async_copy(src, dst, t_sem.at[i]) for i, (src, dst) in enumerate(pairs)]
 
     def weight_copies():
         copies = []
@@ -86,15 +97,18 @@
             copies.append((wd_hbm.at[pl.ds(pl.multiple_of(owner * 192, 64), 192)], wd_sc.at[pl.ds(slot * 192, 192)]))
         return [pltpu.make_async_copy(src, dst, w_sem.at[i]) for i, (src, dst) in enumerate(copies)]
 
-    def norm_row(r):
+    def norm_piece(i):
+        r, _ = piece(i)
+        first = pl.multiple_of(lax.rem(i, 2) * HALF, HALF)
         gamma = gamma_ref[...].astype(F32).reshape(1, HID)
         beta = beta_ref[...].astype(F32).reshape(1, HID)
-        for t in range(0, PART, 32):
-            wide = own[r, pl.ds(t, 32), :].astype(F32)
+        for t in range(0, HALF, 32):
+            rows = pl.ds(first + t, 32)
+            wide = own[r, rows, :].astype(F32)
             mean = jnp.sum(wide, axis=-1, keepdims=True) * (1.0 / HID)
             cent = wide - mean
             var = jnp.sum(cent * cent, axis=-1, keepdims=True) * (1.0 / HID)
-            own[r, pl.ds(t, 32), :] = (cent * lax.rsqrt(var + LN_EPS) * gamma + beta).astype(BF16)
+            own[r, rows, :] = (cent * lax.rsqrt(var + LN_EPS) * gamma + beta).astype(BF16)
 
     def spread_bias():
         for group, owner in enumerate((me, peer_x)):
@@ -105,40 +119,49 @@
 
     @pl.when(step == 0)
     def _():
+        small = small_copies()
+        for c in small[:2]:
+            c.start()
+
         def fetch(r, c):
             load_hidden(r).start()
             return c
 
         lax.fori_loop(0, ROWS, fetch, 0)
-        for c in weight_copies():
-            c.start()
         barrier = pltpu.get_barrier_semaphore()
         for peer in (peer_x, peer_d, peer_xd):
             pl.semaphore_signal(barrier, inc=1, device_id={'sp': peer}, device_id_type=MESH)
+        for c in small[2:] + weight_copies():
+            c.start()
+        for c in small[:2]:
+            c.wait()
+        load_hidden(0).wait()
+        norm_piece(0)
         pl.semaphore_wait(barrier, 3)
+
+        def norm_and_send(i, c):
+            @pl.when(lax.rem(i, 2) == 0)
+            def _():
+                load_hidden(lax.div(i, 2)).wait()
+
+            norm_piece(i)
+            send_x(i - 1).start()
+            return c
+
+        lax.fori_loop(1, 2 * ROWS, norm_and_send, 0)
+        for c in small[2:]:
+            c.wait()
         for n, peer in enumerate((peer_x, peer_d, peer_xd)):
             swap_pos(n, peer).start()
+        send_d(0).start()
         posr[me] = pos_ref[:, 128:256]
-
-        def norm_and_send(r, c):
-            load_hidden(r).wait()
-            norm_row(r)
-
-            @pl.when(r > 0)
-            def _():
-                send_x(r - 1).start()
-
-            return c
-
-        lax.fori_loop(0, ROWS, norm_and_send, 0)
-        send_d(0).start()
         qbd[...] = jnp.zeros_like(qbd)
         spread_bias()
         for c in weight_copies():
             c.wait()
         for n, peer in enumerate((peer_x, peer_d, peer_xd)):
             recv_pos(n, peer).wait()
-        send_x(ROWS - 1).start()
+        send_x(2 * ROWS - 1).start()
 
     def build_tables(r):
         tcos = tcos_ref[...]
@@ -165,10 +188,10 @@
         y_ref[0:rows] = nt_dot(w_sc[0:rows // HEAD].reshape(rows, HID), tokens)
 
     def finish(y_ref, part, with_q):
-        for lt in range(PART // 128):
-            cols = pl.ds(pl.multiple_of(part * PART + lt * 128, 128), 128)
-            ycols = slice(lt * 128, lt * 128 + 128)
-            for h in range(LOCAL):
+        for h in range(LOCAL):
+            for lt in range(PART // 128):
+                cols = pl.ds(pl.multiple_of(part * PART + lt * 128, 128), 128)
+                ycols = slice(lt * 128, lt * 128 + 128)
                 for half in range(2):
                     cos = ctab[16 * half:16 * half + 16, cols]
                     sin = stab[16 * half:16 * half + 16, cols]
@@ -181,10 +204,10 @@
                         w = (y_ref[u0 + 16:u0 + 32, ycols] + bias[b0 + 16:b0 + 32]).astype(BF16).astype(F32)
                         return (u * cos - w * sin).astype(BF16), (w * cos + u * sin).astype(BF16)
 
-                    k0 = h * HEAD + half * 32
+                    k0 = (h % 2) * HEAD + half * 32
                     ku, kw = rotated(0)
-                    kt[k0:k0 + 16, cols] = ku
-                    kt[k0 + 16:k0 + 32, cols] = kw
+                    kt_refs[h // 2][k0:k0 + 16, cols] = ku
+                    kt_refs[h // 2][k0 + 16:k0 + 32, cols] = kw
                     if with_q:
                         qu, qw = rotated(2 * WIDE)
                         q0 = (h % 2) * HEAD + half * 32
@@ -222,39 +245,34 @@
                     top = peak if top is None else jnp.maximum(top, peak)
                 top_sc[2 * j + qb] = jnp.broadcast_to(jnp.max(top, axis=0, keepdims=True) * EXP_SCALE, (8, PART))
 
-        def weigh(j):
-            for qb in range(2):
-                key_len = spec[qb][0]
-                top = top_sc[2 * j + qb, 0:1]
-                total = jnp.zeros((8, PART), F32)
-                for k0 in range(0, key_len, CHUNK):
-                    prob = jnp.exp2(s_refs[2 * j + qb][k0:k0 + CHUNK] * EXP_SCALE - top)
-                    total = total + jnp.sum(prob.reshape(CHUNK // 8, 8, PART), axis=0)
-                    p_refs[2 * j + qb][k0:k0 + CHUNK] = prob.astype(BF16)
-                inv_sc[2 * j + qb] = jnp.broadcast_to(1.0 / jnp.sum(total, axis=0, keepdims=True), (8, PART))
-
         def mix(pair, j):
             v_rows = pl.ds(pl.multiple_of((2 * pair + j) * HEAD, HEAD), HEAD)
             for qb in range(2):
-                key_len = spec[qb][0]
-                mixed = jnp.dot(vt[v_rows, 0:key_len], p_refs[2 * j + qb][0:key_len], preferred_element_type=F32)
-                ctx_buf[lax.rem(r, 2), qb, v_rows, :] = (mixed * inv_sc[2 * j + qb, 0:1]).astype(BF16)
+                top = top_sc[2 * j + qb, 0:1]
+                total = jnp.zeros((8, PART), F32)
+                mixed = None
+                for k0 in range(0, spec[qb][0], MIX):
+                    probs = []
+                    for k1 in range(k0, k0 + MIX, CHUNK):
+                        prob = jnp.exp2(s_refs[2 * j + qb][k1:k1 + CHUNK] * EXP_SCALE - top)
+                        total = total + jnp.sum(prob.reshape(CHUNK // 8, 8, PART), axis=0)
+                        probs.append(prob.astype(BF16))
+                    some = jnp.dot(vt[v_rows, k0:k0 + MIX], jnp.concatenate(probs, axis=0), preferred_element_type=F32)
+                    mixed = some if mixed is None else mixed + some
+                inv = 1.0 / jnp.sum(total, axis=0, keepdims=True)
+                ctx_buf[lax.rem(r, 2), qb, v_rows, :] = (mixed * inv).astype(BF16)
 
         score(0, 0)
-        score(0, 1)
-        weigh(0)
 
         def one_pair(pair, c):
+            score(pair, 1)
+            mix(pair, 0)
             score(pair + 1, 0)
-            weigh(1)
-            mix(pair, 0)
-            score(pair + 1, 1)
-            weigh(0)
             mix(pair, 1)
             return c
 
         lax.fori_loop(0, LOCAL // 2 - 1, one_pair, 0)
-        weigh(1)
+        score(LOCAL // 2 - 1, 1)
         mix(LOCAL // 2 - 1, 0)
         mix(LOCAL // 2 - 1, 1)
 
@@ -270,8 +288,9 @@
 
     @pl.when(step < ROWS)
     def _():
-        send_x(step).wait_recv()
-        relay(step).start()
+        for n in range(2):
+            send_x(2 * step + n).wait_recv()
+            relay(2 * step + n).start()
         build_tables(step)
         send_d(step).wait_recv()
         project(own[step], me, dbuf[lax.rem(step, 2)], peer_d, True)
@@ -283,7 +302,8 @@
 
     @pl.when(step < ROWS)
     def _():
-        relay(step).wait_recv()
+        for n in range(2):
+            relay(2 * step + n).wait_recv()
 
     @pl.when(step < ROWS - 1)
     def _():
@@ -291,26 +311,31 @@
 
     @pl.when(step < ROWS)
     def _():
-        project(xbuf[step], peer_x, rbuf[lax.rem(step, 2)], peer_xd, False)
-        ko_ref[step] = kt[0:192].reshape(3, HEAD, SEQ)
-        vo_ref[step] = vt[0:192].reshape(3, HEAD, SEQ)
+        multiply(y_0, xbuf[step], 2 * WIDE)
+        multiply(y_1, rbuf[lax.rem(step, 2)], 2 * WIDE)
+
+    def rest(r, this_chip):
+        finish(y_0, peer_x, False)
+        finish(y_1, peer_xd, False)
+        ko_ref[r, 0:2] = kt_0[...].reshape(2, HEAD, SEQ)
+        ko_ref[r, 2] = kt_1[0:HEAD]
+        vo_ref[r] = vt[0:192].reshape(3, HEAD, SEQ)
         for pair in range(LOCAL // 2):
-            kk[pair] = kt[pair * 128:(pair + 1) * 128, :].T
-
-    @pl.when(jnp.logical_and(step < ROWS, chip == 0))
-    def _():
-        attend(step, 0)
-
-    @pl.when(jnp.logical_and(step < ROWS, chip == 1))
-    def _():
-        attend(step, 1)
+            kk[pair] = kt_refs[pair][...].T
+        attend(r, this_chip)
+
+    for this_chip in range(2):
+        @pl.when(jnp.logical_and(step < ROWS, chip == this_chip))
+        def _():
+            rest(step, this_chip)
 
     @pl.when(step == ROWS)
     def _():
         def drain(r, c):
-            send_x(r).wait_send()
+            for n in range(2):
+                send_x(2 * r + n).wait_send()
+                relay(2 * r + n).wait_send()
             send_d(r).wait_send()
-            relay(r).wait_send()
             return c
 
         lax.fori_loop(0, ROWS, drain, 0)
@@ -334,9 +359,6 @@
     def local_block(hidden, pos_ids, block_ids, ctx_len, ln_gamma, ln_beta, w_qkv, b_qkv, w_dense, b_dense):
         w_t = jnp.transpose(w_qkv, (1, 2, 3, 0))
         anywhere = pl.BlockSpec(memory_space=pl.ANY)
-
-        def whole(shape):
-            return pl.BlockSpec(shape, lambda i: (0,) * len(shape))
 
         out, keys_t, values_t = pl.pallas_call(
             kernel,
@@ -346,13 +368,16 @@
                 pltpu.VMEM((ROWS, 3, HEAD, SEQ), BF16),
                 pltpu.VMEM((ROWS, 3, HEAD, SEQ), BF16),
             ),
-            in_specs=[
-                anywhere, whole((ROWS, PART)), pl.BlockSpec(memory_space=pltpu.SMEM),
-                whole((HID,)), whole((HID,)), whole((HID,)),
-                anywhere, whole((12, 3, HEAD)), anywhere, whole((16, SEQ)), whole((16, SEQ)),
-            ],
+            in_specs=[anywhere, anywhere, pl.BlockSpec(memory_space=pltpu.SMEM)] + [anywhere] * 8,
             out_specs=(pl.BlockSpec(memory_space=pltpu.VMEM),) * 3,
             scratch_shapes=[
+                pltpu.VMEM((ROWS, PART), jnp.int32),
+                pltpu.VMEM((HID,), BF16),
+                pltpu.VMEM((HID,), BF16),
+                pltpu.VMEM((HID,), BF16),
+                pltpu.VMEM((12, 3, HEAD), BF16),
+                pltpu.VMEM((16, SEQ), F32),
+                pltpu.VMEM((16, SEQ), F32),
                 pltpu.VMEM((ROWS, PART, HID), BF16),
                 pltpu.VMEM((ROWS, PART, HID), BF16),
                 pltpu.VMEM((2, PART, HID), BF16),
@@ -363,21 +388,20 @@
                 pltpu.VMEM((HID, HID), BF16),
                 pltpu.VMEM((3 * WIDE, PART), F32),
                 pltpu.VMEM((3 * WIDE, PART), F32),
-                pltpu.VMEM((WIDE, SEQ), BF16),
+                *[pltpu.VMEM((2 * HEAD, SEQ), BF16)] * 3,
                 pltpu.VMEM((WIDE, SEQ), BF16),
                 pltpu.VMEM((3, SEQ, 128), BF16),
                 pltpu.VMEM((3, 128, 2 * CHIP), BF16),
                 pltpu.VMEM((32, SEQ), F32),
                 pltpu.VMEM((32, SEQ), F32),
                 *[pltpu.VMEM((SEQ, PART), F32)] * 4,
-                *[pltpu.VMEM((SEQ, PART), BF16)] * 4,
-                pltpu.VMEM((4, 8, PART), F32),
                 pltpu.VMEM((4, 8, PART), F32),
                 pltpu.VMEM((2, 2, WIDE, PART), BF16),
                 pltpu.VMEM((2, WIDE, PART), BF16),
+                pltpu.SemaphoreType.DMA((7,)),
                 pltpu.SemaphoreType.DMA((ROWS,)),
                 pltpu.SemaphoreType.DMA((22,)),
-            ] + [pltpu.SemaphoreType.DMA((ROWS,))] * 8 + [pltpu.SemaphoreType.DMA((3,))] * 2,
+            ] + [pltpu.SemaphoreType.DMA((n * ROWS,)) for n in (2, 2, 1, 1, 2, 2, 1, 1)] + [pltpu.SemaphoreType.DMA((3,))] * 2,
             compiler_params=pltpu.CompilerParams(
                 collective_id=0, has_side_effects=True, vmem_limit_bytes=43 * 1024 * 1024, dimension_semantics=('arbitrary',)),
             name='glm_block',

time: 160 us -> 256 us (1.60)
  Pallas kernels: 159 us -> 255 us
    pallas_call x1, Pallas kernels: 152 us -> 249 us  [local_block(): pl.pallas_call(kernel, grid=(ROWS + 1,), out_shape=(pltpu.VMEM((ROWS, PAR...]
where the time goes in v4:
time: 256 us
  Pallas kernels  255 us (100%)
    pallas_call x1, Pallas kernels, local_block(): pl.pallas_call(kernel, grid=(ROWS + 1,), out_shape=(pltpu.VMEM((ROWS, PAR...  249 us
    pallas_call x1, Pallas kernels, local_block(): pl.pallas_call(put, out_shape=[jax.ShapeDtypeStruct(x.shape, BF16) for x...  6.69 us

profile of v4, /device:TPU:0, one launch (start us, length us, event | category | flops | bytes accessed | tf_op | source)
XLA Modules:
  0.0 256.0 jit_solution(13826134589812617557)
XLA Ops:
  0.6 248.6 %glm_block.1 = (bf16[16,256,768]{2,1,0:T(8,128)(2,1)S(1)}, bf16[16,3,64,1024]{3,2,1,0:T(8,128)(2,1)S(1)}, bf16[16,3,64,1024]{3,2,1,0:T(8,128)(2,1)S(1)}) custom-call(bf16[16,256,768]{2,1,0:T(8,128)(2,1)} %hid_hbm.1, s32[16,256]{1,0:T(8,128)} %pos_hbm.1, s32[16]{0:T(128)} %ctx_ref.1, bf16[768]{0:T(1024)(128)(2,1)} %gamma_hbm.1, bf16[768]{0:T(1024)(128)(2,1)} %beta_hbm.1, ...), custom_call_target="tpu_custom_call" | custom-call | tf_op jit(solution)/shard_map/glm_block/pallas_call | solution.py:363
  249.3 6.7 %put.1 = (bf16[16,256,768]{2,1,0:T(8,128)(2,1)}, bf16[16,3,64,1024]{3,2,1,0:T(8,128)(2,1)}, bf16[16,3,64,1024]{3,2,1,0:T(8,128)(2,1)}) custom-call(bf16[16,256,768]{2,1,0:T(8,128)(2,1)S(1)} %get-tuple-element.9.out_vm, bf16[16,3,64,1024]{3,2,1,0:T(8,128)(2,1)S(1)} %get-tuple-element.10.keys_vm, bf16[16,3,64,1024]{3,2,1,0:T(8,128)(2,1)S(1)} %get-tuple-element.11.values_vm), custom_call_target="tpu_custom_call" | custom-call | tf_op jit(solution)/shard_map/put/pallas_call | solution.py:411

commit v5 on v4

--- a/solution.py
+++ b/solution.py
@@ -19,6 +19,7 @@
 ROWS = 16
 PART = 256
 HALF = 128
+AHEAD = 4
 SEQ = 1024
 HID = 768
 HEAD = 64
@@ -145,7 +146,11 @@
                 load_hidden(lax.div(i, 2)).wait()
 
             norm_piece(i)
-            send_x(i - 1).start()
+
+            @pl.when(i <= 2 * AHEAD)
+            def _():
+                send_x(i - 1).start()
+
             return c
 
         lax.fori_loop(1, 2 * ROWS, norm_and_send, 0)
@@ -161,7 +166,6 @@
             c.wait()
         for n, peer in enumerate((peer_x, peer_d, peer_xd)):
             recv_pos(n, peer).wait()
-        send_x(2 * ROWS - 1).start()
 
     def build_tables(r):
         tcos = tcos_ref[...]
@@ -291,6 +295,14 @@
         for n in range(2):
             send_x(2 * step + n).wait_recv()
             relay(2 * step + n).start()
+
+    @pl.when(step < ROWS - AHEAD)
+    def _():
+        for n in range(2):
+            send_x(2 * (step + AHEAD) + n).start()
+
+    @pl.when(step < ROWS)
+    def _():
         build_tables(step)
         send_d(step).wait_recv()
         project(own[step], me, dbuf[lax.rem(step, 2)], peer_d, True)

time: 256 us -> 162 us (0.63)
  Pallas kernels: 255 us -> 161 us
    pallas_call x1, Pallas kernels: 249 us -> 155 us  [local_block(): pl.pallas_call(kernel, grid=(ROWS + 1,), out_shape=(pltpu.VMEM((ROWS, PAR...]
where the time goes in v5:
time: 162 us
  Pallas kernels  161 us (99%)
    pallas_call x1, Pallas kernels, local_block(): pl.pallas_call(kernel, grid=(ROWS + 1,), out_shape=(pltpu.VMEM((ROWS, PAR...  155 us
    pallas_call x1, Pallas kernels, local_block(): pl.pallas_call(put, out_shape=[jax.ShapeDtypeStruct(x.shape, BF16) for x...  6.69 us

profile of v5, /device:TPU:0, one launch (start us, length us, event | category | flops | bytes accessed | tf_op | source)
XLA Modules:
  0.0 161.9 jit_solution(12990635034445719470)
XLA Ops:
  0.6 154.6 %glm_block.1 = (bf16[16,256,768]{2,1,0:T(8,128)(2,1)S(1)}, bf16[16,3,64,1024]{3,2,1,0:T(8,128)(2,1)S(1)}, bf16[16,3,64,1024]{3,2,1,0:T(8,128)(2,1)S(1)}) custom-call(bf16[16,256,768]{2,1,0:T(8,128)(2,1)} %hid_hbm.1, s32[16,256]{1,0:T(8,128)} %pos_hbm.1, s32[16]{0:T(128)} %ctx_ref.1, bf16[768]{0:T(1024)(128)(2,1)} %gamma_hbm.1, bf16[768]{0:T(1024)(128)(2,1)} %beta_hbm.1, ...), custom_call_target="tpu_custom_call" | custom-call | tf_op jit(solution)/shard_map/glm_block/pallas_call | solution.py:375
  155.2 6.7 %put.1 = (bf16[16,256,768]{2,1,0:T(8,128)(2,1)}, bf16[16,3,64,1024]{3,2,1,0:T(8,128)(2,1)}, bf16[16,3,64,1024]{3,2,1,0:T(8,128)(2,1)}) custom-call(bf16[16,256,768]{2,1,0:T(8,128)(2,1)S(1)} %get-tuple-element.9.out_vm, bf16[16,3,64,1024]{3,2,1,0:T(8,128)(2,1)S(1)} %get-tuple-element.10.keys_vm, bf16[16,3,64,1024]{3,2,1,0:T(8,128)(2,1)S(1)} %get-tuple-element.11.values_vm), custom_call_target="tpu_custom_call" | custom-call | tf_op jit(solution)/shard_map/put/pallas_call | solution.py:423

commit v6 on v5

--- a/solution.py
+++ b/solution.py
@@ -18,7 +18,6 @@
 
 ROWS = 16
 PART = 256
-HALF = 128
 AHEAD = 4
 SEQ = 1024
 HID = 768
@@ -58,19 +57,14 @@
     def remote(src, dst, send_sem, recv_sem, peer):
         return pltpu.make_async_remote_copy(src, dst, send_sem, recv_sem, device_id={'sp': peer}, device_id_type=MESH)
 
-    def piece(i):
-        return lax.div(i, 2), pl.ds(pl.multiple_of(lax.rem(i, 2) * HALF, HALF), HALF)
-
-    def send_x(i):
-        r, rows = piece(i)
-        return remote(own.at[r, rows], xbuf.at[r, rows], xs_sem.at[i], xr_sem.at[i], peer_x)
+    def send_x(r):
+        return remote(own.at[r], xbuf.at[r], xs_sem.at[r], xr_sem.at[r], peer_x)
 
     def send_d(r):
         return remote(own.at[r], dbuf.at[lax.rem(r, 2)], ds_sem.at[r], dr_sem.at[r], peer_d)
 
-    def relay(i):
-        r, rows = piece(i)
-        return remote(xbuf.at[r, rows], rbuf.at[lax.rem(r, 2), rows], rs_sem.at[i], rr_sem.at[i], peer_d)
+    def relay(r):
+        return remote(xbuf.at[r], rbuf.at[lax.rem(r, 2)], rs_sem.at[r], rr_sem.at[r], peer_d)
 
     def swap_ctx(r):
         return remote(ctx_buf.at[lax.rem(r, 2), 1 - core], ctx_recv.at[lax.rem(r, 2)], cs_sem.at[r], cr_sem.at[r], peer_d)
@@ -98,13 +92,11 @@
             copies.append((wd_hbm.at[pl.ds(pl.multiple_of(owner * 192, 64), 192)], wd_sc.at[pl.ds(slot * 192, 192)]))
         return [pltpu.make_async_copy(src, dst, w_sem.at[i]) for i, (src, dst) in enumerate(copies)]
 
-    def norm_piece(i):
-        r, _ = piece(i)
-        first = pl.multiple_of(lax.rem(i, 2) * HALF, HALF)
+    def norm_row(r):
         gamma = gamma_ref[...].astype(F32).reshape(1, HID)
         beta = beta_ref[...].astype(F32).reshape(1, HID)
-        for t in range(0, HALF, 32):
-            rows = pl.ds(first + t, 32)
+        for t in range(0, PART, 32):
+            rows = pl.ds(t, 32)
             wide = own[r, rows, :].astype(F32)
             mean = jnp.sum(wide, axis=-1, keepdims=True) * (1.0 / HID)
             cent = wide - mean
@@ -137,23 +129,23 @@
         for c in small[:2]:
             c.wait()
         load_hidden(0).wait()
-        norm_piece(0)
+        norm_row(0)
         pl.semaphore_wait(barrier, 3)
-
-        def norm_and_send(i, c):
-            @pl.when(lax.rem(i, 2) == 0)
+        load_hidden(1).wait()
+        norm_row(1)
+        send_x(0).start()
+
+        def norm_and_send(r, c):
+            load_hidden(r).wait()
+            norm_row(r)
+
+            @pl.when(r <= AHEAD)
             def _():
-                load_hidden(lax.div(i, 2)).wait()
-
-            norm_piece(i)
-
-            @pl.when(i <= 2 * AHEAD)
-            def _():
-                send_x(i - 1).start()
+                send_x(r - 1).start()
 
             return c
 
-        lax.fori_loop(1, 2 * ROWS, norm_and_send, 0)
+        lax.fori_loop(2, ROWS, norm_and_send, 0)
         for c in small[2:]:
             c.wait()
         for n, peer in enumerate((peer_x, peer_d, peer_xd)):
@@ -292,14 +284,12 @@
 
     @pl.when(step < ROWS)
     def _():
-        for n in range(2):
-            send_x(2 * step + n).wait_recv()
-            relay(2 * step + n).start()
+        send_x(step).wait_recv()
+        relay(step).start()
 
     @pl.when(step < ROWS - AHEAD)
     def _():
-        for n in range(2):
-            send_x(2 * (step + AHEAD) + n).start()
+        send_x(step + AHEAD).start()
 
     @pl.when(step < ROWS)
     def _():
@@ -314,8 +304,7 @@
 
     @pl.when(step < ROWS)
     def _():
-        for n in range(2):
-            relay(2 * step + n).wait_recv()
+        relay(step).wait_recv()
 
     @pl.when(step < ROWS - 1)
     def _():
@@ -344,9 +333,8 @@
     @pl.when(step == ROWS)
     def _():
         def drain(r, c):
-            for n in range(2):
-                send_x(2 * r + n).wait_send()
-                relay(2 * r + n).wait_send()
+            send_x(r).wait_send()
+            relay(r).wait_send()
             send_d(r).wait_send()
             return c
 
@@ -413,7 +401,7 @@
                 pltpu.SemaphoreType.DMA((7,)),
                 pltpu.SemaphoreType.DMA((ROWS,)),
                 pltpu.SemaphoreType.DMA((22,)),
-            ] + [pltpu.SemaphoreType.DMA((n * ROWS,)) for n in (2, 2, 1, 1, 2, 2, 1, 1)] + [pltpu.SemaphoreType.DMA((3,))] * 2,
+            ] + [pltpu.SemaphoreType.DMA((ROWS,))] * 8 + [pltpu.SemaphoreType.DMA((3,))] * 2,
             compiler_params=pltpu.CompilerParams(
                 collective_id=0, has_side_effects=True, vmem_limit_bytes=43 * 1024 * 1024, dimension_semantics=('arbitrary',)),
             name='glm_block',

time: 162 us -> 161 us (level)
  no operation moved by 1% of the time
where the time goes in v6:
time: 161 us
  Pallas kernels  160 us (99%)
    pallas_call x1, Pallas kernels, local_block(): pl.pallas_call(kernel, grid=(ROWS + 1,), out_shape=(pltpu.VMEM((ROWS, PAR...  153 us
    pallas_call x1, Pallas kernels, local_block(): pl.pallas_call(put, out_shape=[jax.ShapeDtypeStruct(x.shape, BF16) for x...  6.69 us

profile of v6, /device:TPU:0, one launch (start us, length us, event | category | flops | bytes accessed | tf_op | source)
XLA Modules:
  0.0 160.8 jit_solution(2823400688976049487)
XLA Ops:
  0.6 153.5 %glm_block.1 = (bf16[16,256,768]{2,1,0:T(8,128)(2,1)S(1)}, bf16[16,3,64,1024]{3,2,1,0:T(8,128)(2,1)S(1)}, bf16[16,3,64,1024]{3,2,1,0:T(8,128)(2,1)S(1)}) custom-call(bf16[16,256,768]{2,1,0:T(8,128)(2,1)} %hid_hbm.1, s32[16,256]{1,0:T(8,128)} %pos_hbm.1, s32[16]{0:T(128)} %ctx_ref.1, bf16[768]{0:T(1024)(128)(2,1)} %gamma_hbm.1, bf16[768]{0:T(1024)(128)(2,1)} %beta_hbm.1, ...), custom_call_target="tpu_custom_call" | custom-call | tf_op jit(solution)/shard_map/glm_block/pallas_call | solution.py:363
  154.1 6.7 %put.1 = (bf16[16,256,768]{2,1,0:T(8,128)(2,1)}, bf16[16,3,64,1024]{3,2,1,0:T(8,128)(2,1)}, bf16[16,3,64,1024]{3,2,1,0:T(8,128)(2,1)}) custom-call(bf16[16,256,768]{2,1,0:T(8,128)(2,1)S(1)} %get-tuple-element.9.out_vm, bf16[16,3,64,1024]{3,2,1,0:T(8,128)(2,1)S(1)} %get-tuple-element.10.keys_vm, bf16[16,3,64,1024]{3,2,1,0:T(8,128)(2,1)S(1)} %get-tuple-element.11.values_vm), custom_call_target="tpu_custom_call" | custom-call | tf_op jit(solution)/shard_map/put/pallas_call | solution.py:411

commit v7 on v6

v7 whole, which is shorter than its diff:
```python
import functools
import math

import jax
import jax.numpy as jnp
import numpy as np
from jax import lax
from jax.experimental import pallas as pl
from jax.experimental.pallas import tpu as pltpu
from jax.sharding import PartitionSpec as P

ALPHA = math.sqrt(56.0)
ROPE_BASE = 10000.0
LN_EPS = 1e-5
MESH = pl.DeviceIdType.MESH
F32 = jnp.float32
BF16 = jnp.bfloat16

ROWS = 16
PART = 256
AHEAD = 4
SEQ = 1024
LAST = ROWS - 1
HID = 768
HEAD = 64
CHIP = 512
LOCAL = 6
WIDE = LOCAL * HEAD
EXP_SCALE = math.log2(math.e) / math.sqrt(HEAD)
CHUNK = 64
MIX = 256


def rope_tables():
    freq = ROPE_BASE ** (-np.arange(0, 32, 2).astype(np.float64) / 32.0)
    angle = freq.astype(np.float32)[:, None] * np.arange(SEQ, dtype=np.float32)[None, :]
    return np.cos(angle.astype(np.float64)).astype(np.float32), np.sin(angle.astype(np.float64)).astype(np.float32)


def nt_dot(a, b):
    return lax.dot_general(a, b, (((1,), (1,)), ((), ())), preferred_element_type=F32)


def multiply(y_ref, w_ref, base, rows, tokens):
    y_ref[0:rows] = nt_dot(w_ref[base:base + rows // HEAD].reshape(rows, HID), tokens)


def finish(y_ref, b_ref, base, part, q_col, ctab, stab, kt_refs, vt, qbd):
    for h in range(LOCAL):
        for lt in range(PART // 128):
            cols = pl.ds(pl.multiple_of(part * PART + lt * 128, 128), 128)
            ycols = slice(lt * 128, lt * 128 + 128)
            for half in range(2):
                cos = ctab[16 * half:16 * half + 16, cols]
                sin = stab[16 * half:16 * half + 16, cols]

                def rotated(kind):
                    u0 = kind * WIDE + h * HEAD + half * 32
                    b0 = half * 32
                    bias = b_ref.at[base + kind * LOCAL + h]
                    u = (y_ref[u0:u0 + 16, ycols] + bias[b0:b0 + 16]).astype(BF16).astype(F32)
                    w = (y_ref[u0 + 16:u0 + 32, ycols] + bias[b0 + 16:b0 + 32]).astype(BF16).astype(F32)
                    return (u * cos - w * sin).astype(BF16), (w * cos + u * sin).astype(BF16)

                k0 = (h % 2) * HEAD + half * 32
                ku, kw = rotated(0)
                kt_refs[h // 2][k0:k0 + 16, cols] = ku
                kt_refs[h // 2][k0 + 16:k0 + 32, cols] = kw
                if q_col is not None:
                    qu, qw = rotated(2)
                    q_width = qbd.shape[2] // 2
                    qc = pl.ds(pl.multiple_of((h % 2) * q_width + q_col + lt * 128, 128), 128)
                    qbd[h // 2, k0:k0 + 16, qc] = qu
                    qbd[h // 2, k0 + 16:k0 + 32, qc] = qw
            v0 = WIDE + h * HEAD
            vt[h * HEAD:(h + 1) * HEAD, cols] = (y_ref[v0:v0 + HEAD, ycols] + b_ref[base + LOCAL + h]).astype(BF16)


def attend(spec, q_first, ctx, kk, qbd, vt, s_refs, top_sc, store):
    def score(pair, j):
        for qb, (key_len, mask_from) in enumerate(spec):
            q0 = (j * len(spec) + qb) * PART
            scores = jnp.dot(kk[pair, 0:key_len, :], qbd[pair, :, q0:q0 + PART], preferred_element_type=F32)
            q_pos = q_first + qb * PART + lax.broadcasted_iota(jnp.int32, (1, PART), 1)
            limit = jnp.maximum(q_pos, ctx - 1)
            top = None
            for k0 in range(0, key_len, CHUNK):
                part = scores[k0:k0 + CHUNK]
                if k0 >= mask_from:
                    k_pos = k0 + lax.broadcasted_iota(jnp.int32, (CHUNK, PART), 0)
                    part = jnp.where(k_pos <= limit, part, -jnp.inf)
                s_refs[2 * j + qb][k0:k0 + CHUNK] = part
                peak = jnp.max(part.reshape(CHUNK // 8, 8, PART), axis=0)
                top = peak if top is None else jnp.maximum(top, peak)
            top_sc[2 * j + qb] = jnp.broadcast_to(jnp.max(top, axis=0, keepdims=True) * EXP_SCALE, (8, PART))

    def mix(pair, j):
        v_rows = pl.ds(pl.multiple_of((2 * pair + j) * HEAD, HEAD), HEAD)
        for qb, (key_len, _) in enumerate(spec):
            top = top_sc[2 * j + qb, 0:1]
            total = jnp.zeros((8, PART), F32)
            mixed = None
            for k0 in range(0, key_len, MIX):
                probs = []
                for k1 in range(k0, k0 + MIX, CHUNK):
                    prob = jnp.exp2(s_refs[2 * j + qb][k1:k1 + CHUNK] * EXP_SCALE - top)
                    total = total + jnp.sum(prob.reshape(CHUNK // 8, 8, PART), axis=0)
                    probs.append(prob.astype(BF16))
                some = jnp.dot(vt[v_rows, k0:k0 + MIX], jnp.concatenate(probs, axis=0), preferred_element_type=F32)
                mixed = some if mixed is None else mixed + some
            store(qb, v_rows, (mixed * (1.0 / jnp.sum(total, axis=0, keepdims=True))).astype(BF16))

    score(0, 0)

    def one_pair(pair, c):
        score(pair, 1)
        mix(pair, 0)
        score(pair + 1, 0)
        mix(pair, 1)
        return c

    lax.fori_loop(0, LOCAL // 2 - 1, one_pair, 0)
    score(LOCAL // 2 - 1, 1)
    mix(LOCAL // 2 - 1, 0)
    mix(LOCAL // 2 - 1, 1)


def project_out(mixed, wd, normed, bd_ref):
    dense_out = lax.dot_general(mixed, wd, (((0,), (0,)), ((), ())), preferred_element_type=F32)
    return (normed.astype(F32) * ALPHA + dense_out + bd_ref[...].astype(F32).reshape(1, HID)).astype(BF16)


def kernel(hid_hbm, pos_hbm, ctx_ref, gamma_hbm, beta_hbm, bd_hbm, w_hbm, bias_hbm, wd_hbm, tcos_hbm, tsin_hbm,
           out_ref, ko_ref, vo_ref, a_last, w_sc, b_sc, wd_sc, ctab, stab,
           pos_ref, gamma_ref, beta_ref, bd_ref, bias_ref, tcos_ref, tsin_ref, own, xbuf, dbuf, rbuf, posr, y_0, y_1, kt_0, kt_1, kt_2, vt, kk, qbd, s_0, s_1, s_2, s_3, top_sc, ctx_buf, ctx_recv,
           t_sem, hid_sem, w_sem, xs_sem, xr_sem, ds_sem, dr_sem, rs_sem, rr_sem, cs_sem, cr_sem, ps_sem, pr_sem):
    step = pl.program_id(0)
    s_refs, kt_refs = (s_0, s_1, s_2, s_3), (kt_0, kt_1, kt_2)
    me = lax.axis_index('sp')
    core = lax.rem(me, 2)
    chip = me // 2
    other = 1 - chip
    peer_x = other * 2 + core
    peer_d = chip * 2 + 1 - core
    peer_xd = other * 2 + 1 - core

    def remote(src, dst, send_sem, recv_sem, peer):
        return pltpu.make_async_remote_copy(src, dst, send_sem, recv_sem, device_id={'sp': peer}, device_id_type=MESH)

    def send_x(r):
        return remote(own.at[r], xbuf.at[r], xs_sem.at[r], xr_sem.at[r], peer_x)

    def send_d(r):
        return remote(own.at[r], dbuf.at[lax.rem(r, 2)], ds_sem.at[r], dr_sem.at[r], peer_d)

    def relay(r):
        return remote(xbuf.at[r], rbuf.at[lax.rem(r, 2)], rs_sem.at[r], rr_sem.at[r], peer_d)

    def swap_ctx(r):
        return remote(ctx_buf.at[lax.rem(r, 2), 1 - core], ctx_recv.at[lax.rem(r, 2)], cs_sem.at[r], cr_sem.at[r], peer_d)

    def swap_pos(n, peer):
        return remote(pos_ref.at[:, pl.ds(128, 128)], posr.at[me], ps_sem.at[n], pr_sem.at[n], peer)

    def recv_pos(n, peer):
        return remote(pos_ref.at[:, pl.ds(128, 128)], posr.at[peer], ps_sem.at[n], pr_sem.at[n], peer)

    def load_hidden(r):
        return pltpu.make_async_copy(hid_hbm.at[r], own.at[r], hid_sem.at[r])

    def small_copies():
        pairs = ((gamma_hbm, gamma_ref), (beta_hbm, beta_ref), (pos_hbm, pos_ref), (bd_hbm, bd_ref), (bias_hbm, bias_ref), (tcos_hbm, tcos_ref), (tsin_hbm, tsin_ref))
        return [pltpu.make_async_copy(src, dst, t_sem.at[i]) for i, (src, dst) in enumerate(pairs)]

    def weight_copies():
        copies = []
        for group, owner in enumerate((me, peer_x, peer_d, peer_xd)):
            for slot, kind in ((0, 1), (6, 2), (12, 0)):
                copies.append((w_hbm.at[pl.ds(owner * 3, 3), kind], w_sc.at[pl.ds(18 * (group // 2) + slot + 3 * (group % 2), 3)]))
        for slot, owner in enumerate((me, peer_x, peer_d, peer_xd)):
            copies.append((wd_hbm.at[pl.ds(pl.multiple_of(owner * 192, 64), 192)], wd_sc.at[pl.ds(slot * 192, 192)]))
        return [pltpu.make_async_copy(src, dst, w_sem.at[i]) for i, (src, dst) in enumerate(copies)]

    def norm_row(r):
        gamma = gamma_ref[...].astype(F32).reshape(1, HID)
        beta = beta_ref[...].astype(F32).reshape(1, HID)
        for t in range(0, PART, 32):
            rows = pl.ds(t, 32)
            wide = own[r, rows, :].astype(F32)
            mean = jnp.sum(wide, axis=-1, keepdims=True) * (1.0 / HID)
            cent = wide - mean
            var = jnp.sum(cent * cent, axis=-1, keepdims=True) * (1.0 / HID)
            own[r, rows, :] = (cent * lax.rsqrt(var + LN_EPS) * gamma + beta).astype(BF16)

    def spread_bias():
        for group, owner in enumerate((me, peer_x, peer_d, peer_xd)):
            for slot, kind in ((0, 1), (6, 2), (12, 0)):
                for h in range(3):
                    row = bias_ref[owner * 3 + h, kind:kind + 1, :].astype(F32)
                    b_sc[18 * (group // 2) + slot + 3 * (group % 2) + h] = jnp.broadcast_to(row, (128, HEAD)).T

    @pl.when(step == 0)
    def _():
        small = small_copies()
        for c in small[:2]:
            c.start()

        def fetch(r, c):
            load_hidden(r).start()
            return c

        lax.fori_loop(0, ROWS, fetch, 0)
        barrier = pltpu.get_barrier_semaphore()
        for peer in (peer_x, peer_d, peer_xd):
            pl.semaphore_signal(barrier, inc=1, device_id={'sp': peer}, device_id_type=MESH)
        for c in small[2:] + weight_copies():
            c.start()
        for c in small[:2]:
            c.wait()
        load_hidden(0).wait()
        norm_row(0)
        pl.semaphore_wait(barrier, 3)
        load_hidden(1).wait()
        norm_row(1)
        send_x(0).start()

        def norm_and_send(r, c):
            load_hidden(r).wait()
            norm_row(r)

            @pl.when(r <= AHEAD)
            def _():
                send_x(r - 1).start()

            return c

        lax.fori_loop(2, ROWS, norm_and_send, 0)
        for c in small[2:]:
            c.wait()
        for n, peer in enumerate((peer_x, peer_d, peer_xd)):
            swap_pos(n, peer).start()
        send_d(0).start()
        posr[me] = pos_ref[:, 128:256]
        qbd[...] = jnp.zeros_like(qbd)
        spread_bias()
        for c in weight_copies():
            c.wait()
        for n, peer in enumerate((peer_x, peer_d, peer_xd)):
            recv_pos(n, peer).wait()

    def build_tables(r):
        tcos = tcos_ref[...]
        tsin = tsin_ref[...]
        lane = lax.broadcasted_iota(jnp.int32, (16, SEQ), 1)
        ctx = ctx_ref[r]
        last = posr[3, pl.ds(r, 1), :]
        last_lane = lax.broadcasted_iota(jnp.int32, (1, 128), 1)
        m_pos = jnp.sum(jnp.where(last_lane == 127, last, 0), axis=1, keepdims=True)

        def pick(table, hit):
            return jnp.sum(jnp.where(hit, table, 0.0), axis=1, keepdims=True)

        at_m = lane == m_pos
        at_c = lane == ctx - 1
        in_ctx = lane < ctx
        cos_c, sin_c = pick(tcos, at_c), pick(tsin, at_c)
        ctab[0:16] = jnp.where(in_ctx, tcos, pick(tcos, at_m))
        stab[0:16] = jnp.where(in_ctx, tsin, pick(tsin, at_m))
        ctab[16:32] = jnp.where(in_ctx, 1.0, tcos * cos_c + tsin * sin_c)
        stab[16:32] = jnp.where(in_ctx, 0.0, tsin * cos_c - tcos * sin_c)

    def dense(r):
        mixed = jnp.concatenate([ctx_buf[lax.rem(r, 2), core], ctx_recv[lax.rem(r, 2)]], axis=0)
        out_ref[r] = project_out(mixed, wd_sc[...], own[r], bd_ref)

    @pl.when(step > 0)
    def _():
        swap_ctx(step - 1).start()

    @pl.when(step < ROWS)
    def _():
        send_x(step).wait_recv()
        relay(step).start()

    @pl.when(step < ROWS - AHEAD)
    def _():
        send_x(step + AHEAD).start()

    @pl.when(step < ROWS)
    def _():
        build_tables(step)
        send_d(step).wait_recv()

    @pl.when(step < LAST)
    def _():
        multiply(y_0, w_sc, 0, 3 * WIDE, own[step])
        multiply(y_1, w_sc, 0, 3 * WIDE, dbuf[lax.rem(step, 2)])
        finish(y_0, b_sc, 0, me, core * PART, ctab, stab, kt_refs, vt, qbd)
        finish(y_1, b_sc, 0, peer_d, (1 - core) * PART, ctab, stab, kt_refs, vt, qbd)

    @pl.when(step == LAST)
    def _():
        a_last[me] = own[LAST]
        a_last[peer_d] = dbuf[LAST % 2]

    @pl.when(step > 0)
    def _():
        swap_ctx(step - 1).wait()
        dense(step - 1)

    @pl.when(step < ROWS)
    def _():
        relay(step).wait_recv()

    @pl.when(step < ROWS - 1)
    def _():
        send_d(step + 1).start()

    @pl.when(step < LAST)
    def _():
        multiply(y_0, w_sc, 0, 2 * WIDE, xbuf[step])
        multiply(y_1, w_sc, 0, 2 * WIDE, rbuf[lax.rem(step, 2)])

    def rest(r, this_chip):
        finish(y_0, b_sc, 0, peer_x, None, ctab, stab, kt_refs, vt, qbd)
        finish(y_1, b_sc, 0, peer_xd, None, ctab, stab, kt_refs, vt, qbd)
        ko_ref[r, 0:2] = kt_0[...].reshape(2, HEAD, SEQ)
        ko_ref[r, 2] = kt_1[0:HEAD]
        vo_ref[r] = vt[0:192].reshape(3, HEAD, SEQ)
        for pair in range(LOCAL // 2):
            kk[pair] = kt_refs[pair][...].T

        def store(qb, v_rows, value):
            ctx_buf[lax.rem(r, 2), qb, v_rows, :] = value

        spec = ((768, 256), (768, 256)) if this_chip == 0 else ((768, 512), (1024, 768))
        attend(spec, this_chip * CHIP, ctx_ref[r], kk, qbd, vt, s_refs, top_sc, store)

    for this_chip in range(2):
        @pl.when(jnp.logical_and(step < LAST, chip == this_chip))
        def _():
            rest(step, this_chip)

    @pl.when(step == LAST)
    def _():
        a_last[peer_x] = xbuf[LAST]
        a_last[peer_xd] = rbuf[LAST % 2]

        def drain(r, c):
            send_x(r).wait_send()
            relay(r).wait_send()
            send_d(r).wait_send()
            return c

        lax.fori_loop(0, ROWS, drain, 0)


def last_row(ctx_ref, bd_hbm, out_vm, keys_vm, values_vm, a_last, w_sc, b_sc, wd_sc, ctab, stab,
             out_hbm, keys_hbm, values_hbm,
             bd_ref, y_0, y_1, y_2, y_3, kt_0, kt_1, kt_2, vt, kk, qbd, s_0, s_2, top_sc, ctx_buf, out_row, key_row, value_row, sem, row_sem):
    me = lax.axis_index('sp')
    bulk = []
    for i, (src, dst) in enumerate(((keys_vm, keys_hbm), (values_vm, values_hbm), (out_vm, out_hbm))):
        for n in range(3):
            bulk.append(pltpu.make_async_copy(src.at[pl.ds(5 * n, 5)], dst.at[pl.ds(5 * n, 5)], sem.at[3 * i + n]))
    bd_copy = pltpu.make_async_copy(bd_hbm, bd_ref, row_sem.at[3])
    bd_copy.start()
    for c in bulk:
        c.start()
    kt_refs = (kt_0, kt_1, kt_2)
    s_refs = (s_0, None, s_2, None)
    qbd[...] = jnp.zeros_like(qbd)
    row_copies = [pltpu.make_async_copy(src, dst.at[LAST], row_sem.at[i]) for i, (src, dst) in enumerate(((out_row, out_hbm), (key_row, keys_hbm), (value_row, values_hbm)))]
    for group in range(2):
        base = 3 * LOCAL * group
        parts = [me] + [lax.rem(me + n, 4) for n in range(1, 4)]
        y_refs = (y_0, y_1, y_2, y_3)
        for n in range(4):
            multiply(y_refs[n], w_sc, base, 3 * WIDE if n == 0 else 2 * WIDE, a_last[parts[n]])
        for n in range(4):
            finish(y_refs[n], b_sc, base, parts[n], 0 if n == 0 else None, ctab, stab, kt_refs, vt, qbd)
        if group == 0:
            key_row[0:2] = kt_0[...].reshape(2, HEAD, SEQ)
            key_row[2] = kt_1[0:HEAD]
            value_row[...] = vt[0:192].reshape(3, HEAD, SEQ)
        for pair in range(LOCAL // 2):
            kk[pair] = kt_refs[pair][...].T

        def store(qb, v_rows, value):
            ctx_buf[group, v_rows, :] = value

        for live, spec in ((me < 2, (768, 256)), (me == 2, (768, 512)), (me == 3, (1024, 768))):
            @pl.when(live)
            def _():
                attend((spec,), me * PART, ctx_ref[LAST], kk, qbd, vt, s_refs, top_sc, store)

        if group == 0:
            row_copies[1].start()
            row_copies[2].start()
    bd_copy.wait()
    out_row[...] = project_out(ctx_buf[...].reshape(HID, PART), wd_sc[...], a_last[me], bd_ref)
    row_copies[0].start()
    for c in bulk + row_copies:
        c.wait()


def solution(mesh):
    seq_spec = P('dp', 'sp', None)
    row_spec = P('dp', 'sp')
    head_spec = P('dp', None, 'sp', None)
    replicated = P()
    tcos, tsin = rope_tables()

    def local_block(hidden, pos_ids, block_ids, ctx_len, ln_gamma, ln_beta, w_qkv, b_qkv, w_dense, b_dense):
        w_t = jnp.transpose(w_qkv, (1, 2, 3, 0))
        anywhere = pl.BlockSpec(memory_space=pltpu.HBM)

        held = pl.pallas_call(
            kernel,
            grid=(ROWS,),
            out_shape=(
                pltpu.VMEM((ROWS, PART, HID), BF16),
                pltpu.VMEM((ROWS, 3, HEAD, SEQ), BF16),
                pltpu.VMEM((ROWS, 3, HEAD, SEQ), BF16),
                pltpu.VMEM((4, PART, HID), BF16),
                pltpu.VMEM((36, HEAD, HID), BF16),
                pltpu.VMEM((36, HEAD, 128), F32),
                pltpu.VMEM((HID, HID), BF16),
                pltpu.VMEM((32, SEQ), F32),
                pltpu.VMEM((32, SEQ), F32),
            ),
            in_specs=[anywhere, anywhere, pl.BlockSpec(memory_space=pltpu.SMEM)] + [anywhere] * 8,
            out_specs=(pl.BlockSpec(memory_space=pltpu.VMEM),) * 9,
            scratch_shapes=[
                pltpu.VMEM((ROWS, PART), jnp.int32),
                pltpu.VMEM((HID,), BF16),
                pltpu.VMEM((HID,), BF16),
                pltpu.VMEM((HID,), BF16),
                pltpu.VMEM((12, 3, HEAD), BF16),
                pltpu.VMEM((16, SEQ), F32),
                pltpu.VMEM((16, SEQ), F32),
                pltpu.VMEM((ROWS, PART, HID), BF16),
                pltpu.VMEM((ROWS, PART, HID), BF16),
                pltpu.VMEM((2, PART, HID), BF16),
                pltpu.VMEM((2, PART, HID), BF16),
                pltpu.VMEM((4, ROWS, 128), jnp.int32),
                pltpu.VMEM((3 * WIDE, PART), F32),
                pltpu.VMEM((3 * WIDE, PART), F32),
                *[pltpu.VMEM((2 * HEAD, SEQ), BF16)] * 3,
                pltpu.VMEM((WIDE, SEQ), BF16),
                pltpu.VMEM((3, SEQ, 128), BF16),
                pltpu.VMEM((3, 128, 2 * CHIP), BF16),
                *[pltpu.VMEM((SEQ, PART), F32)] * 4,
                pltpu.VMEM((4, 8, PART), F32),
                pltpu.VMEM((2, 2, WIDE, PART), BF16),
                pltpu.VMEM((2, WIDE, PART), BF16),
                pltpu.SemaphoreType.DMA((7,)),
                pltpu.SemaphoreType.DMA((ROWS,)),
                pltpu.SemaphoreType.DMA((16,)),
            ] + [pltpu.SemaphoreType.DMA((ROWS,))] * 8 + [pltpu.SemaphoreType.DMA((3,))] * 2,
            compiler_params=pltpu.CompilerParams(
                collective_id=0, has_side_effects=True, vmem_limit_bytes=34 * 1024 * 1024, dimension_semantics=('arbitrary',)),
            name='glm_block',
        )(hidden, pos_ids, ctx_len, ln_gamma, ln_beta, b_dense,
          w_t, b_qkv, w_dense, jnp.asarray(tcos), jnp.asarray(tsin))
        held = [pltpu.with_memory_space_constraint(x, pltpu.VMEM) for x in held]
        out, keys_t, values_t = pl.pallas_call(
            last_row,
            out_shape=[jax.ShapeDtypeStruct(x.shape, BF16) for x in held[:3]],
            in_specs=[pl.BlockSpec(memory_space=pltpu.SMEM), anywhere] + [pl.BlockSpec(memory_space=pl.ANY)] * 3 + [pl.BlockSpec(memory_space=pltpu.VMEM)] * 6,
            out_specs=[anywhere] * 3,
            scratch_shapes=[
                pltpu.VMEM((HID,), BF16),
                *[pltpu.VMEM((3 * WIDE, PART), F32)] * 4,
                *[pltpu.VMEM((2 * HEAD, SEQ), BF16)] * 3,
                pltpu.VMEM((WIDE, SEQ), BF16),
                pltpu.VMEM((3, SEQ, 128), BF16),
                pltpu.VMEM((3, 128, 2 * PART), BF16),
                *[pltpu.VMEM((SEQ, PART), F32)] * 2,
                pltpu.VMEM((4, 8, PART), F32),
                pltpu.VMEM((2, WIDE, PART), BF16),
                pltpu.VMEM((PART, HID), BF16),
                pltpu.VMEM((3, HEAD, SEQ), BF16),
                pltpu.VMEM((3, HEAD, SEQ), BF16),
                pltpu.SemaphoreType.DMA((9,)),
                pltpu.SemaphoreType.DMA((4,)),
            ],
            compiler_params=pltpu.CompilerParams(vmem_limit_bytes=34 * 1024 * 1024),
            name='last_row',
        )(ctx_len, b_dense, *held)
        return out, jnp.transpose(keys_t, (0, 3, 1, 2)), jnp.transpose(values_t, (0, 3, 1, 2))

    return jax.shard_map(local_block, mesh=mesh, in_specs=(seq_spec, row_spec, row_spec, P('dp'), replicated, replicated, replicated, replicated, replicated, replicated), out_specs=(seq_spec, head_spec, head_spec), check_vma=False)
```

time: 161 us -> 158 us (0.981)
  Pallas kernels: 160 us -> 157 us
    pallas_call x2, Pallas kernels: 160 us -> 157 us  [the longest x1 146 us: local_block(): pl.pallas_call(kernel, grid=(ROWS,), out_shape=(pltpu.VMEM((ROWS, PART, H...]
where the time goes in v7:
time: 158 us
  Pallas kernels  157 us (99%)
    pallas_call x1, Pallas kernels, local_block(): pl.pallas_call(kernel, grid=(ROWS,), out_shape=(pltpu.VMEM((ROWS, PART, H...  146 us
    pallas_call x1, Pallas kernels, local_block(): pl.pallas_call(last_row, out_shape=[jax.ShapeDtypeStruct(x.shape, BF16) f...  10.5 us

profile of v7, /device:TPU:0, one launch (start us, length us, event | category | flops | bytes accessed | tf_op | source)
XLA Modules:
  0.0 157.6 jit_solution(15510282170607385225)
XLA Ops:
  0.6 146.3 %glm_block.1 = (bf16[16,256,768]{2,1,0:T(8,128)(2,1)S(1)}, bf16[16,3,64,1024]{3,2,1,0:T(8,128)(2,1)S(1)}, bf16[16,3,64,1024]{3,2,1,0:T(8,128)(2,1)S(1)}, bf16[4,...) custom-call(bf16[16,256,768]{2,1,0:T(8,128)(2,1)} %hid_hbm.1, ...), custom_call_target="tpu_custom_call" | custom-call | tf_op jit(solution)/shard_map/glm_block/pallas_call | solution.py:418
  146.9 10.5 %last_row.1 = (bf16[16,256,768]{2,1,0:T(8,128)(2,1)}, bf16[16,3,64,1024]{3,2,1,0:T(8,128)(2,1)}, bf16[16,3,64,1024]{3,2,1,0:T(8,128)(2,1)}) custom-call(s32[16]{0:T(128)} %ctx_ref.3, bf16[768]{0:T(1024)(128)(2,1)} %bd_hbm.3, bf16[16,256,768]{2,1,0:T(8,128)(2,1)S(1)} %get-tuple-element.15.out_vm, bf16[16,3,64,1024]{3,2,1,0:T(8,128)(2,1)S(1)} %get-tuple-element.16.keys_vm, ...), custom_call_target="tpu_custom_call" | custom-call | tf_op jit(solution)/shard_map/last_row/pallas_call | solution.py:467

commit v8 on v7

--- a/solution.py
+++ b/solution.py
@@ -131,7 +131,7 @@
 
 
 def kernel(hid_hbm, pos_hbm, ctx_ref, gamma_hbm, beta_hbm, bd_hbm, w_hbm, bias_hbm, wd_hbm, tcos_hbm, tsin_hbm,
-           out_ref, ko_ref, vo_ref, a_last, w_sc, b_sc, wd_sc, ctab, stab,
+           out_ref, ko_ref, vo_ref, a_last, w_sc, b_sc, wd_sc, ctab, stab, k_last, v_last, q_last,
            pos_ref, gamma_ref, beta_ref, bd_ref, bias_ref, tcos_ref, tsin_ref, own, xbuf, dbuf, rbuf, posr, y_0, y_1, kt_0, kt_1, kt_2, vt, kk, qbd, s_0, s_1, s_2, s_3, top_sc, ctx_buf, ctx_recv,
            t_sem, hid_sem, w_sem, xs_sem, xr_sem, ds_sem, dr_sem, rs_sem, rr_sem, cs_sem, cr_sem, ps_sem, pr_sem):
     step = pl.program_id(0)
@@ -277,22 +277,30 @@
     def _():
         swap_ctx(step - 1).start()
 
-    @pl.when(step < ROWS)
-    def _():
-        send_x(step).wait_recv()
-        relay(step).start()
-
-    @pl.when(step < ROWS - AHEAD)
-    def _():
-        send_x(step + AHEAD).start()
-
-    @pl.when(step < ROWS)
+    @pl.when(step == LAST)
     def _():
         build_tables(step)
         send_d(step).wait_recv()
+        q_last[...] = jnp.zeros_like(q_last)
+        for group in range(2):
+            base = 3 * LOCAL * group
+            multiply(y_0, w_sc, base, 3 * WIDE, own[LAST])
+            multiply(y_1, w_sc, base, 2 * WIDE, dbuf[LAST % 2])
+            last_refs = [k_last.at[group, pair] for pair in range(LOCAL // 2)]
+            finish(y_0, b_sc, base, me, 0, ctab, stab, last_refs, v_last.at[group], q_last.at[group])
+            finish(y_1, b_sc, base, peer_d, None, ctab, stab, last_refs, v_last.at[group], None)
+
+    send_x(step).wait_recv()
+    relay(step).start()
+
+    @pl.when(step < ROWS - AHEAD)
+    def _():
+        send_x(step + AHEAD).start()
 
     @pl.when(step < LAST)
     def _():
+        build_tables(step)
+        send_d(step).wait_recv()
         multiply(y_0, w_sc, 0, 3 * WIDE, own[step])
         multiply(y_1, w_sc, 0, 3 * WIDE, dbuf[lax.rem(step, 2)])
         finish(y_0, b_sc, 0, me, core * PART, ctab, stab, kt_refs, vt, qbd)
@@ -300,8 +308,12 @@
 
     @pl.when(step == LAST)
     def _():
-        a_last[me] = own[LAST]
-        a_last[peer_d] = dbuf[LAST % 2]
+        a_last[0] = own[LAST]
+        multiply(y_0, w_sc, 0, 2 * WIDE, xbuf[LAST])
+        multiply(y_1, w_sc, 3 * LOCAL, 2 * WIDE, xbuf[LAST])
+        for group in range(2):
+            last_refs = [k_last.at[group, pair] for pair in range(LOCAL // 2)]
+            finish((y_0, y_1)[group], b_sc, 3 * LOCAL * group, peer_x, None, ctab, stab, last_refs, v_last.at[group], None)
 
     @pl.when(step > 0)
     def _():
@@ -343,8 +355,7 @@
 
     @pl.when(step == LAST)
     def _():
-        a_last[peer_x] = xbuf[LAST]
-        a_last[peer_xd] = rbuf[LAST % 2]
+        a_last[1] = rbuf[LAST % 2]
 
         def drain(r, c):
             send_x(r).wait_send()
@@ -355,9 +366,9 @@
         lax.fori_loop(0, ROWS, drain, 0)
 
 
-def last_row(ctx_ref, bd_hbm, out_vm, keys_vm, values_vm, a_last, w_sc, b_sc, wd_sc, ctab, stab,
+def last_row(ctx_ref, bd_hbm, out_vm, keys_vm, values_vm, a_last, w_sc, b_sc, wd_sc, ctab, stab, k_last, v_last, q_last,
              out_hbm, keys_hbm, values_hbm,
-             bd_ref, y_0, y_1, y_2, y_3, kt_0, kt_1, kt_2, vt, kk, qbd, s_0, s_2, top_sc, ctx_buf, out_row, key_row, value_row, sem, row_sem):
+             bd_ref, y_0, y_1, kt_0, kt_1, kt_2, vt, kk, s_0, s_2, top_sc, ctx_buf, out_row, key_row, value_row, sem, row_sem):
     me = lax.axis_index('sp')
     bulk = []
     for i, (src, dst) in enumerate(((keys_vm, keys_hbm), (values_vm, values_hbm), (out_vm, out_hbm))):
@@ -369,16 +380,15 @@
         c.start()
     kt_refs = (kt_0, kt_1, kt_2)
     s_refs = (s_0, None, s_2, None)
-    qbd[...] = jnp.zeros_like(qbd)
     row_copies = [pltpu.make_async_copy(src, dst.at[LAST], row_sem.at[i]) for i, (src, dst) in enumerate(((out_row, out_hbm), (key_row, keys_hbm), (value_row, values_hbm)))]
+    far = 3 - me
     for group in range(2):
-        base = 3 * LOCAL * group
-        parts = [me] + [lax.rem(me + n, 4) for n in range(1, 4)]
-        y_refs = (y_0, y_1, y_2, y_3)
-        for n in range(4):
-            multiply(y_refs[n], w_sc, base, 3 * WIDE if n == 0 else 2 * WIDE, a_last[parts[n]])
-        for n in range(4):
-            finish(y_refs[n], b_sc, base, parts[n], 0 if n == 0 else None, ctab, stab, kt_refs, vt, qbd)
+        multiply((y_0, y_1)[group], w_sc, 3 * LOCAL * group, 2 * WIDE, a_last[1])
+    for group in range(2):
+        for pair in range(LOCAL // 2):
+            kt_refs[pair][...] = k_last[group, pair]
+        vt[...] = v_last[group]
+        finish((y_0, y_1)[group], b_sc, 3 * LOCAL * group, far, None, ctab, stab, kt_refs, vt, None)
         if group == 0:
             key_row[0:2] = kt_0[...].reshape(2, HEAD, SEQ)
             key_row[2] = kt_1[0:HEAD]
@@ -392,13 +402,13 @@
         for live, spec in ((me < 2, (768, 256)), (me == 2, (768, 512)), (me == 3, (1024, 768))):
             @pl.when(live)
             def _():
-                attend((spec,), me * PART, ctx_ref[LAST], kk, qbd, vt, s_refs, top_sc, store)
+                attend((spec,), me * PART, ctx_ref[LAST], kk, q_last.at[group], vt, s_refs, top_sc, store)
 
         if group == 0:
             row_copies[1].start()
             row_copies[2].start()
     bd_copy.wait()
-    out_row[...] = project_out(ctx_buf[...].reshape(HID, PART), wd_sc[...], a_last[me], bd_ref)
+    out_row[...] = project_out(ctx_buf[...].reshape(HID, PART), wd_sc[...], a_last[0], bd_ref)
     row_copies[0].start()
     for c in bulk + row_copies:
         c.wait()
@@ -422,15 +432,18 @@
                 pltpu.VMEM((ROWS, PART, HID), BF16),
                 pltpu.VMEM((ROWS, 3, HEAD, SEQ), BF16),
                 pltpu.VMEM((ROWS, 3, HEAD, SEQ), BF16),
-                pltpu.VMEM((4, PART, HID), BF16),
+                pltpu.VMEM((2, PART, HID), BF16),
                 pltpu.VMEM((36, HEAD, HID), BF16),
                 pltpu.VMEM((36, HEAD, 128), F32),
                 pltpu.VMEM((HID, HID), BF16),
                 pltpu.VMEM((32, SEQ), F32),
                 pltpu.VMEM((32, SEQ), F32),
+                pltpu.VMEM((2, LOCAL // 2, 2 * HEAD, SEQ), BF16),
+                pltpu.VMEM((2, WIDE, SEQ), BF16),
+                pltpu.VMEM((2, LOCAL // 2, 2 * HEAD, 2 * PART), BF16),
             ),
             in_specs=[anywhere, anywhere, pl.BlockSpec(memory_space=pltpu.SMEM)] + [anywhere] * 8,
-            out_specs=(pl.BlockSpec(memory_space=pltpu.VMEM),) * 9,
+            out_specs=(pl.BlockSpec(memory_space=pltpu.VMEM),) * 12,
             scratch_shapes=[
                 pltpu.VMEM((ROWS, PART), jnp.int32),
                 pltpu.VMEM((HID,), BF16),
@@ -459,7 +472,7 @@
                 pltpu.SemaphoreType.DMA((16,)),
             ] + [pltpu.SemaphoreType.DMA((ROWS,))] * 8 + [pltpu.SemaphoreType.DMA((3,))] * 2,
             compiler_params=pltpu.CompilerParams(
-                collective_id=0, has_side_effects=True, vmem_limit_bytes=34 * 1024 * 1024, dimension_semantics=('arbitrary',)),
+                collective_id=0, has_side_effects=True, vmem_limit_bytes=32 * 1024 * 1024, dimension_semantics=('arbitrary',)),
             name='glm_block',
         )(hidden, pos_ids, ctx_len, ln_gamma, ln_beta, b_dense,
           w_t, b_qkv, w_dense, jnp.asarray(tcos), jnp.asarray(tsin))
@@ -467,15 +480,14 @@
         out, keys_t, values_t = pl.pallas_call(
             last_row,
             out_shape=[jax.ShapeDtypeStruct(x.shape, BF16) for x in held[:3]],
-            in_specs=[pl.BlockSpec(memory_space=pltpu.SMEM), anywhere] + [pl.BlockSpec(memory_space=pl.ANY)] * 3 + [pl.BlockSpec(memory_space=pltpu.VMEM)] * 6,
+            in_specs=[pl.BlockSpec(memory_space=pltpu.SMEM), anywhere] + [pl.BlockSpec(memory_space=pl.ANY)] * 3 + [pl.BlockSpec(memory_space=pltpu.VMEM)] * 9,
             out_specs=[anywhere] * 3,
             scratch_shapes=[
                 pltpu.VMEM((HID,), BF16),
-                *[pltpu.VMEM((3 * WIDE, PART), F32)] * 4,
+                *[pltpu.VMEM((2 * WIDE, PART), F32)] * 2,
                 *[pltpu.VMEM((2 * HEAD, SEQ), BF16)] * 3,
                 pltpu.VMEM((WIDE, SEQ), BF16),
                 pltpu.VMEM((3, SEQ, 128), BF16),
-                pltpu.VMEM((3, 128, 2 * PART), BF16),
                 *[pltpu.VMEM((SEQ, PART), F32)] * 2,
                 pltpu.VMEM((4, 8, PART), F32),
                 pltpu.VMEM((2, WIDE, PART), BF16),
@@ -485,7 +497,7 @@
                 pltpu.SemaphoreType.DMA((9,)),
                 pltpu.SemaphoreType.DMA((4,)),
             ],
-            compiler_params=pltpu.CompilerParams(vmem_limit_bytes=34 * 1024 * 1024),
+            compiler_params=pltpu.CompilerParams(vmem_limit_bytes=32 * 1024 * 1024),
             name='last_row',
         )(ctx_len, b_dense, *held)
         return out, jnp.transpose(keys_t, (0, 3, 1, 2)), jnp.transpose(values_t, (0, 3, 1, 2))

time: 158 us -> 157 us (level)
    pallas_call x1, Pallas kernels: 10.5 us -> 7.92 us  [local_block(): pl.pallas_call(last_row, out_shape=[jax.ShapeDtypeStruct(x.shape, BF16) f...]
where the time goes in v8:
time: 157 us; the launch traced here: 156 us
  Pallas kernels  156 us (99%)
    pallas_call x1, Pallas kernels, local_block(): pl.pallas_call(kernel, grid=(ROWS,), out_shape=(pltpu.VMEM((ROWS, PART, H...  148 us
    pallas_call x1, Pallas kernels, local_block(): pl.pallas_call(last_row, out_shape=[jax.ShapeDtypeStruct(x.shape, BF16) f...  7.92 us

profile of v8, /device:TPU:0, one launch (start us, length us, event | category | flops | bytes accessed | tf_op | source)
XLA Modules:
  0.0 156.4 jit_solution(5910361885233662490)
XLA Ops:
  0.6 147.7 %glm_block.1 = (bf16[16,256,768]{2,1,0:T(8,128)(2,1)S(1)}, bf16[16,3,64,1024]{3,2,1,0:T(8,128)(2,1)S(1)}, bf16[16,3,64,1024]{3,2,1,0:T(8,128)(2,1)S(1)}, bf16[2,...) custom-call(bf16[16,256,768]{2,1,0:T(8,128)(2,1)} %hid_hbm.1, ...), custom_call_target="tpu_custom_call" | custom-call | tf_op jit(solution)/shard_map/glm_block/pallas_call | solution.py:428
  148.3 7.9 %last_row.1 = (bf16[16,256,768]{2,1,0:T(8,128)(2,1)}, bf16[16,3,64,1024]{3,2,1,0:T(8,128)(2,1)}, bf16[16,3,64,1024]{3,2,1,0:T(8,128)(2,1)}) custom-call(s32[16]{0:T(128)} %ctx_ref.3, bf16[768]{0:T(1024)(128)(2,1)} %bd_hbm.3, bf16[16,256,768]{2,1,0:T(8,128)(2,1)S(1)} %get-tuple-element.18.out_vm, bf16[16,3,64,1024]{3,2,1,0:T(8,128)(2,1)S(1)} %get-tuple-element.19.keys_vm, ...), custom_call_target="tpu_custom_call" | custom-call | tf_op jit(solution)/shard_map/last_row/pallas_call | solution.py:480

commit v9 on v8

--- a/solution.py
+++ b/solution.py
@@ -153,6 +153,9 @@
     def send_d(r):
         return remote(own.at[r], dbuf.at[lax.rem(r, 2)], ds_sem.at[r], dr_sem.at[r], peer_d)
 
+    def send_d_last():
+        return remote(own.at[LAST], dbuf.at[2], ds_sem.at[LAST], dr_sem.at[LAST], peer_d)
+
     def relay(r):
         return remote(xbuf.at[r], rbuf.at[lax.rem(r, 2)], rs_sem.at[r], rr_sem.at[r], peer_d)
 
@@ -213,16 +216,16 @@
         barrier = pltpu.get_barrier_semaphore()
         for peer in (peer_x, peer_d, peer_xd):
             pl.semaphore_signal(barrier, inc=1, device_id={'sp': peer}, device_id_type=MESH)
-        for c in small[2:] + weight_copies():
-            c.start()
         for c in small[:2]:
             c.wait()
         load_hidden(0).wait()
         norm_row(0)
+        for c in small[2:] + weight_copies():
+            c.start()
         pl.semaphore_wait(barrier, 3)
+        send_x(0).start()
         load_hidden(1).wait()
         norm_row(1)
-        send_x(0).start()
 
         def norm_and_send(r, c):
             load_hidden(r).wait()
@@ -240,6 +243,7 @@
         for n, peer in enumerate((peer_x, peer_d, peer_xd)):
             swap_pos(n, peer).start()
         send_d(0).start()
+        send_d_last().start()
         posr[me] = pos_ref[:, 128:256]
         qbd[...] = jnp.zeros_like(qbd)
         spread_bias()
@@ -277,18 +281,22 @@
     def _():
         swap_ctx(step - 1).start()
 
-    @pl.when(step == LAST)
-    def _():
-        build_tables(step)
-        send_d(step).wait_recv()
+    @pl.when(step == 0)
+    def _():
+        build_tables(LAST)
+        send_d_last().wait_recv()
         q_last[...] = jnp.zeros_like(q_last)
         for group in range(2):
             base = 3 * LOCAL * group
             multiply(y_0, w_sc, base, 3 * WIDE, own[LAST])
-            multiply(y_1, w_sc, base, 2 * WIDE, dbuf[LAST % 2])
+            multiply(y_1, w_sc, base, 2 * WIDE, dbuf[2])
             last_refs = [k_last.at[group, pair] for pair in range(LOCAL // 2)]
             finish(y_0, b_sc, base, me, 0, ctab, stab, last_refs, v_last.at[group], q_last.at[group])
             finish(y_1, b_sc, base, peer_d, None, ctab, stab, last_refs, v_last.at[group], None)
+
+    @pl.when(step == LAST)
+    def _():
+        build_tables(LAST)
 
     send_x(step).wait_recv()
     relay(step).start()
@@ -324,7 +332,7 @@
     def _():
         relay(step).wait_recv()
 
-    @pl.when(step < ROWS - 1)
+    @pl.when(step < LAST - 1)
     def _():
         send_d(step + 1).start()
 
@@ -363,7 +371,10 @@
             send_d(r).wait_send()
             return c
 
-        lax.fori_loop(0, ROWS, drain, 0)
+        lax.fori_loop(0, LAST, drain, 0)
+        send_x(LAST).wait_send()
+        relay(LAST).wait_send()
+        send_d_last().wait_send()
 
 
 def last_row(ctx_ref, bd_hbm, out_vm, keys_vm, values_vm, a_last, w_sc, b_sc, wd_sc, ctab, stab, k_last, v_last, q_last,
@@ -454,7 +465,7 @@
                 pltpu.VMEM((16, SEQ), F32),
                 pltpu.VMEM((ROWS, PART, HID), BF16),
                 pltpu.VMEM((ROWS, PART, HID), BF16),
-                pltpu.VMEM((2, PART, HID), BF16),
+                pltpu.VMEM((3, PART, HID), BF16),
                 pltpu.VMEM((2, PART, HID), BF16),
                 pltpu.VMEM((4, ROWS, 128), jnp.int32),
                 pltpu.VMEM((3 * WIDE, PART), F32),

time: 157 us -> 157 us (level)
  no operation moved by 1% of the time
where the time goes in v9:
time: 157 us
  Pallas kernels  156 us (99%)
    pallas_call x1, Pallas kernels, local_block(): pl.pallas_call(kernel, grid=(ROWS,), out_shape=(pltpu.VMEM((ROWS, PART, H...  149 us
    pallas_call x1, Pallas kernels, local_block(): pl.pallas_call(last_row, out_shape=[jax.ShapeDtypeStruct(x.shape, BF16) f...  7.92 us

profile of v9, /device:TPU:0, one launch (start us, length us, event | category | flops | bytes accessed | tf_op | source)
XLA Modules:
  0.0 157.3 jit_solution(4810429978935292823)
XLA Ops:
  0.6 148.6 %glm_block.1 = (bf16[16,256,768]{2,1,0:T(8,128)(2,1)S(1)}, bf16[16,3,64,1024]{3,2,1,0:T(8,128)(2,1)S(1)}, bf16[16,3,64,1024]{3,2,1,0:T(8,128)(2,1)S(1)}, bf16[2,...) custom-call(bf16[16,256,768]{2,1,0:T(8,128)(2,1)} %hid_hbm.1, ...), custom_call_target="tpu_custom_call" | custom-call | tf_op jit(solution)/shard_map/glm_block/pallas_call | solution.py:439
  149.2 7.9 %last_row.1 = (bf16[16,256,768]{2,1,0:T(8,128)(2,1)}, bf16[16,3,64,1024]{3,2,1,0:T(8,128)(2,1)}, bf16[16,3,64,1024]{3,2,1,0:T(8,128)(2,1)}) custom-call(s32[16]{0:T(128)} %ctx_ref.3, bf16[768]{0:T(1024)(128)(2,1)} %bd_hbm.3, bf16[16,256,768]{2,1,0:T(8,128)(2,1)S(1)} %get-tuple-element.18.out_vm, bf16[16,3,64,1024]{3,2,1,0:T(8,128)(2,1)S(1)} %get-tuple-element.19.keys_vm, ...), custom_call_target="tpu_custom_call" | custom-call | tf_op jit(solution)/shard_map/last_row/pallas_call | solution.py:491

commit v10 on v8

--- a/solution.py
+++ b/solution.py
@@ -18,7 +18,7 @@
 
 ROWS = 16
 PART = 256
-AHEAD = 4
+AHEAD = 15
 SEQ = 1024
 LAST = ROWS - 1
 HID = 768

time: 157 us -> 247 us (1.57)
  Pallas kernels: 156 us -> 246 us
    pallas_call x1, Pallas kernels: 148 us -> 238 us  [local_block(): pl.pallas_call(kernel, grid=(ROWS,), out_shape=(pltpu.VMEM((ROWS, PART, H...]
where the time goes in v10:
time: 247 us; the launch traced here: 246 us
  Pallas kernels  246 us (100%)
    pallas_call x1, Pallas kernels, local_block(): pl.pallas_call(kernel, grid=(ROWS,), out_shape=(pltpu.VMEM((ROWS, PART, H...  238 us
    pallas_call x1, Pallas kernels, local_block(): pl.pallas_call(last_row, out_shape=[jax.ShapeDtypeStruct(x.shape, BF16) f...  7.92 us

profile of v10, /device:TPU:0, one launch (start us, length us, event | category | flops | bytes accessed | tf_op | source)
XLA Modules:
  0.0 246.5 jit_solution(6985393349464726995)
XLA Ops:
  0.6 237.7 %glm_block.1 = (bf16[16,256,768]{2,1,0:T(8,128)(2,1)S(1)}, bf16[16,3,64,1024]{3,2,1,0:T(8,128)(2,1)S(1)}, bf16[16,3,64,1024]{3,2,1,0:T(8,128)(2,1)S(1)}, bf16[2,...) custom-call(bf16[16,256,768]{2,1,0:T(8,128)(2,1)} %hid_hbm.1, ...), custom_call_target="tpu_custom_call" | custom-call | tf_op jit(solution)/shard_map/glm_block/pallas_call | solution.py:428
  238.4 7.9 %last_row.1 = (bf16[16,256,768]{2,1,0:T(8,128)(2,1)}, bf16[16,3,64,1024]{3,2,1,0:T(8,128)(2,1)}, bf16[16,3,64,1024]{3,2,1,0:T(8,128)(2,1)}) custom-call(s32[16]{0:T(128)} %ctx_ref.3, bf16[768]{0:T(1024)(128)(2,1)} %bd_hbm.3, bf16[16,256,768]{2,1,0:T(8,128)(2,1)S(1)} %get-tuple-element.18.out_vm, bf16[16,3,64,1024]{3,2,1,0:T(8,128)(2,1)S(1)} %get-tuple-element.19.keys_vm, ...), custom_call_target="tpu_custom_call" | custom-call | tf_op jit(solution)/shard_map/last_row/pallas_call | solution.py:480

commit v11 on v10

--- a/solution.py
+++ b/solution.py
@@ -18,7 +18,7 @@
 
 ROWS = 16
 PART = 256
-AHEAD = 15
+AHEAD = 2
 SEQ = 1024
 LAST = ROWS - 1
 HID = 768

time: 247 us -> 157 us (0.64)
  Pallas kernels: 246 us -> 156 us
    pallas_call x1, Pallas kernels: 238 us -> 148 us  [local_block(): pl.pallas_call(kernel, grid=(ROWS,), out_shape=(pltpu.VMEM((ROWS, PART, H...]
where the time goes in v11:
time: 157 us; the launch traced here: 156 us
  Pallas kernels  156 us (99%)
    pallas_call x1, Pallas kernels, local_block(): pl.pallas_call(kernel, grid=(ROWS,), out_shape=(pltpu.VMEM((ROWS, PART, H...  148 us
    pallas_call x1, Pallas kernels, local_block(): pl.pallas_call(last_row, out_shape=[jax.ShapeDtypeStruct(x.shape, BF16) f...  7.92 us

profile of v11, /device:TPU:0, one launch (start us, length us, event | category | flops | bytes accessed | tf_op | source)
XLA Modules:
  0.0 156.4 jit_solution(9575384629307532476)
XLA Ops:
  0.6 147.7 %glm_block.1 = (bf16[16,256,768]{2,1,0:T(8,128)(2,1)S(1)}, bf16[16,3,64,1024]{3,2,1,0:T(8,128)(2,1)S(1)}, bf16[16,3,64,1024]{3,2,1,0:T(8,128)(2,1)S(1)}, bf16[2,...) custom-call(bf16[16,256,768]{2,1,0:T(8,128)(2,1)} %hid_hbm.1, ...), custom_call_target="tpu_custom_call" | custom-call | tf_op jit(solution)/shard_map/glm_block/pallas_call | solution.py:428
  148.3 7.9 %last_row.1 = (bf16[16,256,768]{2,1,0:T(8,128)(2,1)}, bf16[16,3,64,1024]{3,2,1,0:T(8,128)(2,1)}, bf16[16,3,64,1024]{3,2,1,0:T(8,128)(2,1)}) custom-call(s32[16]{0:T(128)} %ctx_ref.3, bf16[768]{0:T(1024)(128)(2,1)} %bd_hbm.3, bf16[16,256,768]{2,1,0:T(8,128)(2,1)S(1)} %get-tuple-element.18.out_vm, bf16[16,3,64,1024]{3,2,1,0:T(8,128)(2,1)S(1)} %get-tuple-element.19.keys_vm, ...), custom_call_target="tpu_custom_call" | custom-call | tf_op jit(solution)/shard_map/last_row/pallas_call | solution.py:480
